TPU v7x, 32 devices: a whole 2x2x4 slice. The times are simulated.
32 devices in a mesh: groups: 2 (over x), ep: 8 (over z, y), node: 2 (over core).
Axes of the slice: x: 2, y: 2, z: 4, core: 2. Of those that a mesh axis runs over, the one named last changes fastest.
Arguments:
- tokens: bfloat16 [1024, 7168], P(('groups', 'ep', 'node')), parts along dimension 0, may hold values from -6 to 6
- expert_ids: int32 [1024, 8], P(('groups', 'ep', 'node')), parts along dimension 0, may hold values from 0 to 15, all different within a row; in each aligned block of 32 rows (0 to 31, 32 to 63, ...) at most 32 rows name the same one
- gate_weights: float32 [1024, 8], P(('groups', 'ep', 'node')), parts along dimension 0, may hold values from 0.05 to 0.5
- gate_up_weight: bfloat16 [16, 7168, 512], P(('ep', 'node')), may hold values from -0.0625 to 0.0625
- down_weight: bfloat16 [16, 256, 7168], P(('ep', 'node')), may hold values from -0.375 to 0.375
Outputs:
- moe_out: bfloat16 [1024, 7168], P(('groups', 'ep', 'node')), parts along dimension 0
There are 2 independent parts, one for each index of `groups`. A program takes and returns all parts, laid end to end along the dimension named above; an argument that names none is the same for every part. Nothing has to cross between parts.
Inputs may be any that keep to these rules, and one draw needn't show every extreme that they name: `expert_ids`: each token names 8 different experts; among the 32 tokens of one device no expert is named by more than 32 of them, a bound that some block reaches.
All inputs are finite; a program needn't handle non-finite values.
Results may differ from a plain program's by a relative error of at most 0.0058.
Values may be sent and summed in bfloat16 or wider, within the bound.
A program may use at most 128 MiB of HBM per device.

v0:
```python
import functools

import jax
import jax.numpy as jnp
from jax import lax
from jax.experimental import pallas as pl
from jax.experimental.pallas import tpu as pltpu
from jax.sharding import PartitionSpec as P

AXES = ("ep", "node")
PAIR = 2
PIECES = 2
SIDE = 7
LANES = 128
VMEM_BYTES = 60 * 1024 * 1024
MESH = pl.DeviceIdType.MESH


def spread_out(tokens, expert_ids, gate_weights, gate_up_weight, down_weight):
    local_count, inner_width = down_weight.shape[0], down_weight.shape[1]
    device = lax.axis_index("ep") * lax.axis_size("node") + lax.axis_index("node")
    all_tokens = lax.all_gather(tokens, AXES, axis=0, tiled=True)
    all_ids = lax.all_gather(expert_ids, AXES, axis=0, tiled=True)
    all_weights = lax.all_gather(gate_weights, AXES, axis=0, tiled=True)
    total = 0.0
    for local in range(local_count):
        expert = device * local_count + local
        share = jnp.sum(jnp.where(all_ids == expert, all_weights, 0.0), axis=1)
        gate_up = jnp.dot(all_tokens, gate_up_weight[local], preferred_element_type=jnp.float32)
        hidden = (jax.nn.silu(gate_up[:, :inner_width]) * gate_up[:, inner_width:]).astype(
            jnp.bfloat16
        )
        product = jnp.dot(hidden, down_weight[local], preferred_element_type=jnp.float32)
        total = total + share[:, None] * product
    return lax.psum_scatter(total.astype(jnp.bfloat16), AXES, scatter_dimension=0, tiled=True)


def block_of(width, most):
    return max(b for b in range(LANES, most + 1, LANES) if width % b == 0)


def pick(table, z):
    value = jnp.int32(table[0])
    for k in range(1, len(table)):
        value = jnp.where(z == k, jnp.int32(table[k]), value)
    return value


def near_first(z, line):
    order = [z]
    for d in range(1, line):
        order += [j for j in (z - d, z + d) if 0 <= j < line]
    return order


def send_order(z, line):
    order = near_first(z, line)
    return order[1:2] + order[2:][::-1] + order[:1]


def kernel(
    line, experts, x_ref, wgu_hbm, wd_hbm, out_ref,
    tok, part, near, chain, near_b, chain_b, wg, wd, acc, hid,
    x_sem, up_s, dn_s, y_s, tok_r, w_l, w_s, w_r, n_s, n_r, c_s, c_r,
    up_b, dn_b, y_b, tok_b, nb_s, nb_r, cb_s, cb_r,
):
    rows, width = out_ref.shape
    inner = wd.shape[1]
    main = width - near_b.shape[1]
    side = pl.ds(main, width - main)
    e = lax.axis_index("ep")
    c = lax.axis_index("node")
    z, y = e // PAIR, e % PAIR
    other = 1 - y
    first, last = z == 0, z == line - 1
    has_dn, has_up = z > 0, z < line - 1
    to_up, to_dn = {"ep": e + PAIR}, {"ep": e - PAIR}
    to_y, to_core = {"ep": z * PAIR + other}, {"node": 1 - c}

    barrier = pltpu.get_barrier_semaphore()

    def greet(target):
        pl.semaphore_signal(barrier, inc=1, device_id=target, device_id_type=MESH)

    greet(to_core)
    greet(to_y)
    pl.when(has_up)(lambda: greet(to_up))
    pl.when(has_dn)(lambda: greet(to_dn))
    pl.semaphore_wait(barrier, 2 + jnp.where(has_up, 1, 0) + jnp.where(has_dn, 1, 0))

    def remote(src, dst, s, r, target):
        return pltpu.make_async_remote_copy(
            src_ref=src, dst_ref=dst, send_sem=s, recv_sem=r,
            device_id=target, device_id_type=MESH,
        )

    def tok_copy(j, sems, target, own=False):
        at = pl.ds(0, main)
        src = x_ref.at[:, at] if own else tok.at[j, y, :, at]
        return remote(src, tok.at[j, y, :, at], sems.at[j], tok_r.at[j, y], target)

    def tok_arrived(j, row):
        ref = tok.at[j, row, :, pl.ds(0, main)]
        remote(ref, ref, up_s.at[j], tok_r.at[j, row], to_y).wait_recv()

    def side_copy(j, row, sem, target, own=False):
        at = pl.ds(main, x_ref.shape[1] - main)
        src = x_ref.at[:, at] if own else tok.at[j, row, :, at]
        return remote(src, tok.at[j, row, :, at], sem, tok_b.at[j, row], target)

    def side_up(j, row, own=False):
        return side_copy(j, row, up_b.at[j, row], to_up, own)

    def side_dn(j, row, own=False):
        return side_copy(j, row, dn_b.at[j, row], to_dn, own)

    def forward(d):
        own = d == 0

        def below():
            j = z - d
            if own:
                side_copy(j, y, y_b, to_y, own).start()
            else:
                tok_arrived(j, y)
            pl.when(has_up)(lambda: tok_copy(j, up_s, to_up, own).start())
            if own:
                pl.when(has_dn)(lambda: tok_copy(j, dn_s, to_dn, own).start())
            tok_copy(j, y_s, to_y, own).start()
            for row in (y, other):
                mine = own and row is y
                if not mine:
                    side_up(j, row).wait_recv()
                pl.when(has_up)(lambda: side_up(j, row, mine).start())
                if own:
                    pl.when(has_dn)(lambda: side_dn(j, row, mine).start())

        def above():
            j = z + d
            tok_arrived(j, y)
            pl.when(has_dn)(lambda: tok_copy(j, dn_s, to_dn).start())
            tok_copy(j, y_s, to_y).start()
            for row in (y, other):
                side_dn(j, row).wait_recv()
                pl.when(has_dn)(lambda: side_dn(j, row).start())

        if own:
            below()
        else:
            pl.when(z >= d)(below)
            pl.when(z + d < line)(above)

    own_copy = pltpu.make_async_copy(x_ref, tok.at[z, y], x_sem)
    own_copy.start()
    local = [
        pltpu.make_async_copy(wgu_hbm.at[0], wg.at[0], w_l.at[0]),
        pltpu.make_async_copy(wd_hbm.at[0], wd.at[0], w_l.at[1]),
    ]
    swapped = [
        remote(wgu_hbm.at[0], wg.at[1], w_s.at[0], w_r.at[0], to_core),
        remote(wd_hbm.at[0], wd.at[1], w_s.at[1], w_r.at[1], to_core),
    ]
    for copy in swapped + local:
        copy.start()

    forward(0)
    mine = e * 2 + c
    names = (mine, e * 2 + 1 - c)
    k_block, n_block = block_of(width, 1792), block_of(width, 1024)

    def compute(p):
        j = pick([near_first(k, line)[p] for k in range(line)], z)
        tok_arrived(j, other)
        if p == 0:
            own_copy.wait()
            local[0].wait()
            swapped[0].wait_recv()
        acc[...] = jnp.zeros_like(acc)

        def up_step(k, carry):
            at = pl.ds(pl.multiple_of(k * k_block, k_block), k_block)
            block = tok[j, :, :, at].reshape(PAIR * rows, k_block)
            for s in range(2):
                acc[s] += jnp.dot(block, wg[s, at, :], preferred_element_type=jnp.float32)
            return carry

        lax.fori_loop(0, width // k_block, up_step, 0)
        for s in range(2):
            gate, up = acc[s, :, :inner], acc[s, :, inner:]
            hid[s] = (jax.nn.silu(gate) * up).astype(jnp.bfloat16)
        meta = tok[j, :, :, width:].astype(jnp.float32).reshape(PAIR * rows, -1)
        lane = lax.broadcasted_iota(jnp.int32, meta.shape, 1)
        shares = [
            jnp.sum(
                jnp.where((lane == name) | (lane == name + experts), meta, 0.0),
                axis=1, keepdims=True,
            )
            for name in names
        ]
        if p == 0:
            local[1].wait()
            swapped[1].wait_recv()

        def down_step(n, carry):
            at = pl.ds(pl.multiple_of(n * n_block, n_block), n_block)
            total = 0.0
            for s in range(2):
                total += shares[s] * jnp.dot(
                    hid[s], wd[s, :, at], preferred_element_type=jnp.float32
                )
            part[j, :, :, at] = total.astype(jnp.bfloat16).reshape(PAIR, rows, n_block)
            return carry

        lax.fori_loop(0, width // n_block, down_step, 0)

    piece = main // PIECES

    def near_copy(j, q):
        at = pl.ds(q * piece, piece)
        return remote(
            part.at[j, other, :, at], near.at[j, :, at], n_s.at[j, q], n_r.at[j, q], to_y
        )

    def send_near(p):
        j = pick([send_order(k, line)[p] for k in range(line)], z)
        for q in range(PIECES):
            near_copy(j, q).start()

    for d in range(1, line):
        forward(d)
        if d == line - 1:
            break
        compute(d - 1)
    compute(line - 2)
    send_near(0)
    compute(line - 1)
    for p in range(1, line):
        send_near(p)

    def chain_copy(j, slot, q, target):
        at = pl.ds(q * piece, piece)
        return remote(
            part.at[j, y, :, at], chain.at[slot, :, at], c_s.at[j, q], c_r.at[slot, q], target
        )

    def chain_arrived(slot, q):
        chain_copy(0, slot, q, to_y).wait_recv()

    def chain_up(j, d, q, start):
        copy = chain_copy(j, j, q, to_up)
        copy.start() if start else copy.wait_send()

    def chain_dn(j, d, q, start):
        copy = chain_copy(j, line if d == 1 else j, q, to_dn)
        copy.start() if start else copy.wait_send()

    def hop(j, q, came, push):
        at = pl.ds(q * piece, piece)
        near_copy(j, q).wait_recv()
        pl.when(came)(lambda: chain_arrived(j, q))
        total = part[j, y, :, at].astype(jnp.float32) + near[j, :, at].astype(jnp.float32)

        @pl.when(came)
        def _():
            part[j, y, :, at] = (total + chain[j, :, at].astype(jnp.float32)).astype(jnp.bfloat16)

        @pl.when(jnp.logical_not(came))
        def _():
            part[j, y, :, at] = total.astype(jnp.bfloat16)

        push()

    def side_sum(j, row, d, came, upward, start):
        slot = line if d == 1 and not upward else j
        copy = remote(
            part.at[j, row, :, side], chain_b.at[slot, row], cb_s.at[j, row],
            cb_r.at[slot, row], to_up if upward else to_dn,
        )
        if not start:
            copy.wait_send()
            return

        @pl.when(came)
        def _():
            side_arrived(j, row)
            total = part[j, row, :, side].astype(jnp.float32)
            total += chain_b[j, row].astype(jnp.float32)
            part[j, row, :, side] = total.astype(jnp.bfloat16)

        copy.start()

    def side_arrived(slot, row):
        ref = chain_b.at[slot, row]
        remote(ref, ref, cb_s.at[0, row], cb_r.at[slot, row], to_y).wait_recv()

    def side_total(row):
        pl.when(has_dn)(lambda: side_arrived(z, row))
        pl.when(has_up)(lambda: side_arrived(line, row))
        below, above = chain_b[z, row].astype(jnp.float32), chain_b[line, row].astype(jnp.float32)
        total = part[z, row, :, side].astype(jnp.float32)
        return total + jnp.where(has_dn, below, 0.0) + jnp.where(has_up, above, 0.0)

    side_near = remote(part.at[z, other, :, side], near_b, nb_s, nb_r, to_y)
    for d in range(line - 1, 0, -1):
        for row in range(PAIR):
            pl.when(z + d < line)(functools.partial(
                lambda d, row: side_sum(z + d, row, d, has_dn, True, True), d, row))
            pl.when(z >= d)(functools.partial(
                lambda d, row: side_sum(z - d, row, d, has_up, False, True), d, row))
    part[z, other, :, side] = side_total(other).astype(jnp.bfloat16)
    side_near.start()
    side_total_own = side_total(y)

    for d in range(line - 1, 0, -1):
        for q in range(PIECES):
            pl.when(z + d < line)(functools.partial(
                lambda d, q: hop(z + d, q, has_dn, lambda: chain_up(z + d, d, q, True)), d, q))
            pl.when(z >= d)(functools.partial(
                lambda d, q: hop(z - d, q, has_up, lambda: chain_dn(z - d, d, q, True)), d, q))

    for q in range(PIECES):
        at = pl.ds(q * piece, piece)
        near_copy(z, q).wait_recv()
        pl.when(has_dn)(lambda: chain_arrived(z, q))
        pl.when(has_up)(lambda: chain_arrived(line, q))
        total = part[z, y, :, at].astype(jnp.float32) + near[z, :, at].astype(jnp.float32)
        below = chain[z, :, at].astype(jnp.float32)
        above = chain[line, :, at].astype(jnp.float32)

        @pl.when(has_dn & has_up)
        def _():
            out_ref[:, at] = (total + below + above).astype(jnp.bfloat16)

        @pl.when(first)
        def _():
            out_ref[:, at] = (total + above).astype(jnp.bfloat16)

        @pl.when(last)
        def _():
            out_ref[:, at] = (total + below).astype(jnp.bfloat16)

    side_near.wait_recv()
    out_ref[:, side] = (side_total_own + near_b[...].astype(jnp.float32)).astype(jnp.bfloat16)

    side_near.wait_send()
    side_copy(z, y, y_b, to_y, True).wait_send()
    for copy in swapped:
        copy.wait_send()
    for d in range(line):
        own = d == 0

        def below(d=d, own=own):
            pl.when(has_up)(lambda: tok_copy(z - d, up_s, to_up, own).wait_send())
            for row in range(PAIR):
                pl.when(has_up)(lambda row=row: side_up(z - d, row).wait_send())
                if own:
                    pl.when(has_dn)(lambda row=row: side_dn(z, row).wait_send())
                else:
                    side_sum(z - d, row, d, None, False, False)
            if own:
                pl.when(has_dn)(lambda: tok_copy(z, dn_s, to_dn, own).wait_send())
            else:
                for q in range(PIECES):
                    chain_dn(z - d, d, q, False)
            tok_copy(z - d, y_s, to_y, own).wait_send()
            for q in range(PIECES):
                near_copy(z - d, q).wait_send()

        def above(d=d):
            pl.when(has_dn)(lambda: tok_copy(z + d, dn_s, to_dn).wait_send())
            for row in range(PAIR):
                pl.when(has_dn)(lambda row=row: side_dn(z + d, row).wait_send())
                side_sum(z + d, row, d, None, True, False)
            tok_copy(z + d, y_s, to_y).wait_send()
            for q in range(PIECES):
                chain_up(z + d, d, q, False)
                near_copy(z + d, q).wait_send()

        if own:
            below()
        else:
            pl.when(z >= d)(below)
            pl.when(z + d < line)(above)


def on_grid(line, tokens, expert_ids, gate_weights, gate_up_weight, down_weight):
    experts = lax.axis_size("ep") * lax.axis_size("node")
    rows, width = tokens.shape
    inner = down_weight.shape[1]
    chosen = expert_ids[:, :, None] == jnp.arange(experts, dtype=jnp.int32)
    share = jnp.sum(jnp.where(chosen, gate_weights[:, :, None], 0.0), axis=1)
    high = lax.reduce_precision(share, 8, 7)
    tail = -2 * experts % LANES
    rest = jnp.pad(jnp.concatenate([high, share - high], axis=1), ((0, 0), (0, tail)))
    x = jnp.concatenate([tokens, rest.astype(jnp.bfloat16)], axis=1)
    step = LANES * PIECES
    side = width - (width - width // SIDE) // step * step
    dma, vmem, bf = pltpu.SemaphoreType.DMA, pltpu.VMEM, jnp.bfloat16
    return pl.pallas_call(
        functools.partial(kernel, line, experts),
        out_shape=jax.ShapeDtypeStruct((rows, width), bf),
        in_specs=[
            pl.BlockSpec(memory_space=pltpu.VMEM),
            pl.BlockSpec(memory_space=pl.ANY),
            pl.BlockSpec(memory_space=pl.ANY),
        ],
        out_specs=pl.BlockSpec(memory_space=pltpu.VMEM),
        scratch_shapes=[
            vmem((line, PAIR, rows, x.shape[1]), bf),
            vmem((line, PAIR, rows, width), bf),
            vmem((line, rows, width - side), bf),
            vmem((line + 1, rows, width - side), bf),
            vmem((rows, side), bf),
            vmem((line + 1, PAIR, rows, side), bf),
            vmem((2, width, 2 * inner), bf),
            vmem((2, inner, width), bf),
            vmem((2, PAIR * rows, 2 * inner), jnp.float32),
            vmem((2, PAIR * rows, inner), bf),
            dma(()), dma((line,)), dma((line,)), dma((line,)), dma((line, PAIR)),
            dma((2,)), dma((2,)), dma((2,)),
            dma((line, PIECES)), dma((line, PIECES)),
            dma((line, PIECES)), dma((line + 1, PIECES)),
            dma((line, PAIR)), dma((line, PAIR)), dma(()), dma((line, PAIR)),
            dma(()), dma(()), dma((line, PAIR)), dma((line + 1, PAIR)),
        ],
        compiler_params=pltpu.CompilerParams(
            collective_id=0, has_side_effects=True, vmem_limit_bytes=VMEM_BYTES
        ),
    )(x, gate_up_weight, down_weight)


def on_device(tokens, expert_ids, gate_weights, gate_up_weight, down_weight):
    chips, cores = lax.axis_size("ep"), lax.axis_size("node")
    line = chips // PAIR
    rows, width = tokens.shape
    inner = down_weight.shape[1]
    planes = (5 * line + 2 * PAIR) * rows * width * 2 + 6 * inner * width * 2 * 1.1
    args = (tokens, expert_ids, gate_weights, gate_up_weight, down_weight)
    fits = planes < 0.9 * VMEM_BYTES and gate_up_weight.shape[0] == 1
    paired = cores == 2 and lax.axis_size("groups") * PAIR == 4
    if fits and paired and chips % PAIR == 0 and line > 1:
        return on_grid(line, *args)
    return spread_out(*args)


def solution(mesh):
    placed = (
        P(("groups", "ep", "node"), None),
        P(("groups", "ep", "node"), None),
        P(("groups", "ep", "node"), None),
        P(("ep", "node"), None, None),
        P(("ep", "node"), None, None),
    )
    return jax.shard_map(
        on_device,
        mesh=mesh,
        in_specs=placed,
        out_specs=P(("groups", "ep", "node"), None),
        check_vma=False,
    )
```

profile of v0, /device:TPU:0, one launch (start us, length us, event | category | flops | bytes accessed | tf_op | source)
XLA Modules:
  0.0 95.9 jit_solution(6529663363388185857)
XLA Ops:
  0.0 0.7 select_reduce_fusion
  0.7 0.1 copy.11
  0.8 0.1 copy.10
  0.9 0.1 fusion.2
  1.0 1.8 %pad_maximum_fusion.x_ref = bf16[32,7296]{1,0:T(8,128)(2,1)} fusion(bf16[32,128]{1,0:T(8,128)(2,1)S(1)} %fusion.2, bf16[32,7168]{1,0:T(8,128)(2,1)} %param.5), kind=kLoop, calls=%fused_computation | loop fusion | flops 933888 | bytes 933888 | tf_op jit(solution)/shard_map/concatenate | solution.py:395
  2.8 91.3 %shard_map.55 = bf16[32,7168]{1,0:T(8,128)(2,1)} custom-call(bf16[32,7296]{1,0:T(8,128)(2,1)} %pad_maximum_fusion.x_ref, bf16[1,7168,512]{2,1,0:T(8,128)(2,1)} %wgu_hbm.1, bf16[1,256,7168]{2,1,0:T(8,128)(2,1)} %wd_hbm.1), custom_call_target="tpu_custom_call" | custom-call | tf_op jit(solution)/shard_map/pallas_call | solution.py:399
  94.1 1.8 %copy.14 = bf16[32,7168]{1,0:T(8,128)(2,1)} copy(bf16[32,7168]{1,0:T(8,128)(2,1)} %shard_map.55) | data formatting | bytes 917504
  (2 shorter events, 0.0 us)
where the time goes:
time: 96.2 us; the launch traced here: 95.9 us
  Pallas kernels  91.3 us (95%)
  other arithmetic  2.64 us (3%)
  local copies, waits for them, and re-layouts  1.96 us (2%)
    pallas_call x1, Pallas kernels, on_grid(): pl.pallas_call(functools.partial(kernel, line, experts), out_shape=jax.Sh...  91.3 us

commit v1 on v0

v1 whole, which is shorter than its diff:
```python
import functools

import jax
import jax.numpy as jnp
from jax import lax
from jax.experimental import pallas as pl
from jax.experimental.pallas import tpu as pltpu
from jax.sharding import PartitionSpec as P

AXES = ("ep", "node")
DRAIN_AFTER = 8.0


def spread_out(tokens, expert_ids, gate_weights, gate_up_weight, down_weight):
    local_count, inner_width = down_weight.shape[0], down_weight.shape[1]
    device = lax.axis_index("ep") * lax.axis_size("node") + lax.axis_index("node")
    all_tokens = lax.all_gather(tokens, AXES, axis=0, tiled=True)
    all_ids = lax.all_gather(expert_ids, AXES, axis=0, tiled=True)
    all_weights = lax.all_gather(gate_weights, AXES, axis=0, tiled=True)
    total = 0.0
    for local in range(local_count):
        expert = device * local_count + local
        share = jnp.sum(jnp.where(all_ids == expert, all_weights, 0.0), axis=1)
        gate_up = jnp.dot(all_tokens, gate_up_weight[local], preferred_element_type=jnp.float32)
        hidden = (jax.nn.silu(gate_up[:, :inner_width]) * gate_up[:, inner_width:]).astype(
            jnp.bfloat16
        )
        product = jnp.dot(hidden, down_weight[local], preferred_element_type=jnp.float32)
        total = total + share[:, None] * product
    return lax.psum_scatter(total.astype(jnp.bfloat16), AXES, scatter_dimension=0, tiled=True)


RATE = dict(z=1.405, y=1.405, lat=2.1, up=0.75, dn=0.5, hid=0.4, sum=0.12, op=0.04, w0=11.0, w1=17.0, depth=2.5, meta=0.2)

def rank(style, b, top):
    if style == 'near': return b
    if style == 'far': return top - b
    return 0 if b == 0 else top + 1 - b

def plan(line, pieces, ag, rs, style='nf', cstyle='nf', rate=None, sidefirst=True, own=1.5, tweak=None):
    R = dict(RATE); R.update(rate or {})
    L, P = line, pieces
    META = P
    time_of, waiting, avail, link, clock = {}, {}, [[] for _ in range(L)], {}, [0.0]*L
    order = [[] for _ in range(L)]
    count = 0
    def post(event, t):
        time_of[event] = t
        for op in waiting.pop(event, ()):
            op['need'] -= 1
            op['ready'] = max(op['ready'], t)
            if op['need'] == 0: avail[op['z']].append(op)
    ops = []
    def add(z, name, deps, key, lk=None):
        op = dict(z=z, name=name, need=0, ready=0.0, key=key, link=lk)
        for d in set(deps):
            waiting.setdefault(d, []).append(op); op['need'] += 1
        ops.append(op)
        if op['need'] == 0: avail[z].append(op)
        return op
    sf = (lambda p: -p) if sidefirst else (lambda p: p)
    for z in range(L):
        for j in range(L):
            d = abs(j - z)
            dist = own if d == 0 else d
            crank = rank(cstyle, d-1, L-2) if d else own
            for lk, step, ends in (('u', 1, L-1), ('d', -1, 0)):
                if z == ends or (j - z)*step > 0: continue
                top = z if step > 0 else L-1-z
                a = rank(style, d, top)
                for p in list(range(P)) + [META]:
                    for r in ((0,) if p < ag[j] or p == META else (0, 1)):
                        add(z, ('AGZ', j, r, p, lk), [('t', z, j, r, p)], (0, a, p != META, sf(p), r), lk)
            for p in list(range(P)) + [META]:
                if p < ag[j] or p == META or j == z:
                    add(z, ('AGY', j, 0, p), [('t', z, j, 0, p)], (0, crank if j != z else -1, p != META, sf(p)), 'y')
            for p in range(P):
                add(z, ('UP', j, p), [('t', z, j, 0, p), ('t', z, j, 1, p), ('w0', z)], (3, crank, sf(p)))
                add(z, ('DN', j, p), [('h', z, j), ('w1', z)], (2, crank, sf(p)))
            add(z, ('HID', j), [('a', z, j, p) for p in range(P)] + [('t', z, j, 0, META), ('t', z, j, 1, META)], (2, crank, -99))
            for p in range(rs[j]):
                add(z, ('NEAR', j, p), [('p', z, j, p)], (1, crank, sf(p)), 'y')
            for p in range(P):
                main = p < rs[j]
                for r in ((0,) if main else (1, 0)):
                    deps = [('p', z, j, p)]
                    if j == z:
                        if z > 0: deps.append(('c', z, z, r, p))
                        if z < L-1: deps.append(('c', z, L, r, p))
                        if r == 0: deps.append(('n', z, z, p))
                        add(z, ('FIN', r, p), deps, (1, -1 if r == 1 else 9, sf(p)), 'y' if r == 1 else None)
                    else:
                        if main: deps.append(('n', z, j, p))
                        came = z > 0 if j > z else z < L-1
                        if came: deps.append(('c', z, j, r, p))
                        add(z, ('SUM', j, r, p), deps, (1, crank, sf(p), -r), 'u' if j > z else 'd')
    for z in range(L):
        for lk in 'udy': link[z, lk] = 0.0
        for p in range(P+1): post(('t', z, z, 0, p), 0.0)
        post(('w0', z), R['w0']); post(('w1', z), R['w1'])
    def send(z, lk, t, size):
        e = max(t, link[z, lk]) + size
        link[z, lk] = e
        return e + R['lat']
    left = len(ops)
    while left:
        best = None
        for z in range(L):
            if not avail[z]: continue
            st = min(max(o['ready'], link[z, o['link']] - R['depth']) if o['link'] else o['ready'] for o in avail[z])
            st = max(st, clock[z])
            if best is None or st < best[0]: best = (st, z)
        t, z = best
        cand = [o for o in avail[z] if o['ready'] <= t + 1e-9 and (not o['link'] or link[z, o['link']] - R['depth'] <= t + 1e-9)]
        op = min(cand, key=lambda o: o['key'])
        avail[z].remove(op)
        left -= 1
        n = op['name']; k = n[0]
        if k in ('AGZ', 'AGY'):
            te = t + R['op']
            size = R['meta'] if n[3] == META else R['y' if k == 'AGY' else 'z']
            if k == 'AGY': te2 = send(z, 'y', te, size); post(('t', z, n[1], 1, n[3]), te2)
            else:
                te2 = send(z, n[4], te, size)
                post(('t', z + (1 if n[4] == 'u' else -1), n[1], n[2], n[3]), te2)
        elif k == 'UP':
            te = t + R['up']; post(('a', z, n[1], n[2]), te)
        elif k == 'HID':
            te = t + R['hid']; post(('h', z, n[1]), te)
        elif k == 'DN':
            te = t + R['dn']; post(('p', z, n[1], n[2]), te)
        elif k == 'NEAR':
            te = t + R['op']; post(('n', z, n[1], n[2]), send(z, 'y', te, R['y']))
        elif k == 'SUM':
            te = t + R['sum']; up = n[1] > z; zz = z + (1 if up else -1)
            slot = L if (zz == n[1] and not up) else n[1]
            post(('c', zz, slot, n[2], n[3]), send(z, 'u' if up else 'd', te, R['z']))
        elif k == 'FIN':
            te = t + R['sum']
            if n[1] == 1: post(('n', z, z, n[2]), send(z, 'y', te, R['y']))
        clock[z] = te
        order[z].append((t, te, n))
    return order, max(clock), link


def pieces_of(width):
    return max(n for n in range(1, 8) if width % (n * LANES) == 0)


def splits(line, pieces):
    ends = round(pieces * 5 / 7)
    return (ends,) * line, (ends,) * line


PAIR = 2
LANES = 128
VMEM_BYTES = 60 * 1024 * 1024
MESH = pl.DeviceIdType.MESH
HEAVY = {"NONE": 0, "UP": 1, "HID": 2, "DN": 3, "SUM": 4}
UP_TO, DOWN_TO, SIDE_TO, HERE = 0, 1, 2, 3


def steps_of(line, pieces, ag, rs, order):
    programs = []
    for z in range(line):
        steps, seen, drains = [], set(), []

        def emit(op, j=0, r=0, p=0, dest=0, slot=0, near=0, below=0, above=0):
            steps.append((op, j, r, p, dest, slot, near, below, above))

        def drain(t, *step):
            drains.append((t, step))

        def need(j, r, p):
            if (j, r, p) in seen:
                return
            seen.add((j, r, p))
            if j == z and r == 0:
                if "own" not in seen:
                    seen.add("own")
                    emit("OWN")
            elif p == pieces:
                emit("RTM", j, r)
            else:
                emit("RT", j, r, p)

        def weight(which):
            if which not in seen:
                seen.add(which)
                emit(which)

        for start, end, n in order[z]:
            while drains and drains[0][0] < start - DRAIN_AFTER:
                emit(*drains.pop(0)[1])
            k = n[0]
            if k == "AGZ":
                _, j, r, p, lk = n
                need(j, r, p)
                dest = UP_TO if lk == "u" else DOWN_TO
                slot = line if j == z and dest == DOWN_TO else j
                if p == pieces:
                    emit("AGZM", j, r, 0, dest, slot)
                    drain(start, "DZM", j, r, 0, dest, slot)
                else:
                    emit("AGZ", j, r, p, dest, slot)
                    drain(start, "DZ", j, r, p, dest, slot)
            elif k == "AGY":
                _, j, r, p = n
                need(j, r, p)
                if p == pieces:
                    emit("AGYM", j)
                    drain(start, "DYM", j)
                else:
                    emit("AGY", j, 0, p)
                    drain(start, "DY", j, 0, p)
            elif k == "UP":
                need(n[1], 0, n[2])
                need(n[1], 1, n[2])
                weight("W0")
                emit("UP", n[1], 0, n[2])
            elif k == "HID":
                need(n[1], 0, pieces)
                need(n[1], 1, pieces)
                emit("HID", n[1])
            elif k == "DN":
                weight("W1")
                emit("DN", n[1], 0, n[2])
            elif k == "NEAR":
                emit("NEAR", n[1], 0, n[2])
                drain(start, "DN_S", n[1], 0, n[2])
            elif k == "SUM":
                _, j, r, p = n
                up = j > z
                far = j == z - 1
                came = z > 0 if up else z < line - 1
                dest = UP_TO if up else DOWN_TO
                slot = line if far else j
                emit("SUM", j, r, p, dest, slot, int(p < rs[j]), int(came))
                drain(start, "DC", j, r, p, dest, slot)
            elif k == "FIN":
                _, r, p = n
                dest = SIDE_TO if r == 1 else HERE
                emit("SUM", z, r, p, dest, z, int(r == 0), int(z > 0), int(z < line - 1))
                if r == 1:
                    drain(start, "DN_S", z, 0, p)
        for _, step in drains:
            emit(*step)
        programs.append(grouped(steps))
    longest = max(len(p) for p in programs)
    return [p + [([], ("NONE",))] * (longest - len(p)) for p in programs]


def grouped(steps):
    groups, light = [], []
    for fields in steps:
        if fields[0] in HEAVY:
            groups.append((light, fields))
            light = []
        else:
            light.append(fields)
    return groups + [(light, ("NONE",))]


FIELDS = ((8, "op"), (16, "j"), (2, "r"), (32, "p"), (4, "dest"), (16, "slot"), (2, "near"), (2, "below"), (2, "above"))


def packed(step):
    word, scale = 0, 1
    for (size, _), value in zip(FIELDS, (HEAVY[step[0]],) + tuple(step[1:])):
        word += value * scale
        scale *= size
    return word


def kernel(
    line, pieces, experts, programs, ids_ref, gate_ref, x_hbm, wgu_hbm, wd_hbm, out_ref,
    tok, meta, part, near, chain, wg, wd, acc, hid, share, tot,
    x_sem, w_l, w_s, w_r, tok_r, zs, ys, near_r, near_s, chain_r, chain_s,
):
    rows, width = out_ref.shape
    inner = wd.shape[1]
    block = width // pieces
    e = lax.axis_index("ep")
    c = lax.axis_index("node")
    z, y = e // PAIR, e % PAIR
    other = 1 - y
    has_dn, has_up = z > 0, z < line - 1
    to_up, to_dn = {"ep": e + PAIR}, {"ep": e - PAIR}
    to_y, to_core = {"ep": z * PAIR + other}, {"node": 1 - c}

    own_copy = pltpu.make_async_copy(x_hbm, tok.at[z, y], x_sem)
    own_copy.start()
    local = [
        pltpu.make_async_copy(wgu_hbm.at[0], wg.at[0], w_l.at[0]),
        pltpu.make_async_copy(wd_hbm.at[0], wd.at[0], w_l.at[1]),
    ]
    for copy in local:
        copy.start()

    barrier = pltpu.get_barrier_semaphore()

    def greet(target):
        pl.semaphore_signal(barrier, inc=1, device_id=target, device_id_type=MESH)

    greet(to_core)
    greet(to_y)
    pl.when(has_up)(lambda: greet(to_up))
    pl.when(has_dn)(lambda: greet(to_dn))

    lane = lax.broadcasted_iota(jnp.int32, (rows, LANES), 1)
    name = jnp.where(lane < experts, lane, lane - experts)
    total = jnp.zeros((rows, LANES), jnp.float32)
    for k in range(ids_ref.shape[1]):
        total += jnp.where(ids_ref[:, k : k + 1] == name, gate_ref[:, k : k + 1], 0.0)
    high = total.astype(jnp.bfloat16)
    low = (total - high.astype(jnp.float32)).astype(jnp.bfloat16)
    wide = jnp.where(lane < experts, high.astype(jnp.float32), low.astype(jnp.float32))
    meta[z, y] = jnp.where(lane < 2 * experts, wide, 0.0).astype(jnp.bfloat16)
    acc[...] = jnp.zeros_like(acc)

    pl.semaphore_wait(barrier, 2 + jnp.where(has_up, 1, 0) + jnp.where(has_dn, 1, 0))

    def remote(src, dst, s, r, target):
        return pltpu.make_async_remote_copy(
            src_ref=src, dst_ref=dst, send_sem=s, recv_sem=r,
            device_id=target, device_id_type=MESH,
        )

    swapped = [
        remote(wgu_hbm.at[0], wg.at[1], w_s.at[0], w_r.at[0], to_core),
        remote(wd_hbm.at[0], wd.at[1], w_s.at[1], w_r.at[1], to_core),
    ]
    for copy in swapped:
        copy.start()
    mine = e * 2 + c
    names = (mine, e * 2 + 1 - c)

    def span(p):
        return pl.ds(pl.multiple_of(p * block, LANES), block)

    def tok_copy(j, row, p, s, target):
        ref = tok.at[j, row, :, span(p)]
        return remote(ref, ref, s, tok_r.at[j, row, p], target)

    def meta_copy(j, row, s, target):
        ref = meta.at[j, row]
        return remote(ref, ref, s, tok_r.at[j, row, pieces], target)

    def both_ways(dest, act):
        pl.when(dest == UP_TO)(lambda: act(to_up))
        pl.when(dest == DOWN_TO)(lambda: act(to_dn))

    def near_copy(j, src, p):
        return remote(
            src.at[:, span(p)], near.at[j, :, span(p)], near_s.at[j, p], near_r.at[j, p], to_y
        )

    def chain_copy(j, row, p, slot, target):
        return remote(
            part.at[j, row, :, span(p)], chain.at[slot, row, :, span(p)],
            chain_s.at[j, row, p], chain_r.at[slot, row, p], target,
        )

    def up(j, p):
        at = span(p)
        rows_in = tok[j, :, :, at].reshape(PAIR * rows, block)
        for s in range(2):
            acc[j, s] += jnp.dot(rows_in, wg[s, at, :], preferred_element_type=jnp.float32)

    def hidden(j):
        for s in range(2):
            gate, over = acc[j, s, :, :inner], acc[j, s, :, inner:]
            hid[j, s] = (jax.nn.silu(gate) * over).astype(jnp.bfloat16)
        parts = meta[j].astype(jnp.float32).reshape(PAIR * rows, LANES)
        at = lax.broadcasted_iota(jnp.int32, parts.shape, 1)
        for s, expert in enumerate(names):
            kept = jnp.where((at == expert) | (at == expert + experts), parts, 0.0)
            share[j, s] = jnp.broadcast_to(
                jnp.sum(kept, axis=1, keepdims=True), (PAIR * rows, LANES)
            )

    def down(j, p):
        at = span(p)
        total = 0.0
        for s in range(2):
            product = jnp.dot(hid[j, s], wd[s, :, at], preferred_element_type=jnp.float32)
            total += share[j, s, :, :1] * product
        part[j, :, :, at] = total.astype(jnp.bfloat16).reshape(PAIR, rows, block)

    def sums(j, row, p, dest, slot, f_near, f_below, f_above):
        at = span(p)
        tot[...] = part[j, row, :, at].astype(jnp.float32)

        @pl.when(f_near == 1)
        def _():
            near_copy(j, part.at[j, row], p).wait_recv()
            tot[...] += near[j, :, at].astype(jnp.float32)

        @pl.when(f_below == 1)
        def _():
            chain_copy(j, row, p, j, to_y).wait_recv()
            tot[...] += chain[j, row, :, at].astype(jnp.float32)

        @pl.when(f_above == 1)
        def _():
            chain_copy(j, row, p, line, to_y).wait_recv()
            tot[...] += chain[line, row, :, at].astype(jnp.float32)

        value = tot[...].astype(jnp.bfloat16)

        @pl.when(dest == HERE)
        def _():
            out_ref[:, at] = value

        @pl.when(dest != HERE)
        def _():
            part[j, row, :, at] = value
            both_ways(dest, lambda target: chain_copy(j, row, p, slot, target).start())
            pl.when(dest == SIDE_TO)(lambda: near_copy(j, part.at[j, row], p).start())

    def light(fields):
        name, j, r, p, dest, slot = fields[:6]
        row = other if r else y
        target = to_up if dest == UP_TO else to_dn
        if name == "RT":
            tok_copy(j, row, p, x_sem, to_y).wait_recv()
        elif name == "RTM":
            meta_copy(j, row, x_sem, to_y).wait_recv()
        elif name == "AGZ":
            tok_copy(j, row, p, zs.at[slot, r, p], target).start()
        elif name == "AGZM":
            meta_copy(j, row, zs.at[slot, r, pieces], target).start()
        elif name == "AGY":
            tok_copy(j, y, p, ys.at[j, p], to_y).start()
        elif name == "AGYM":
            meta_copy(j, y, ys.at[j, pieces], to_y).start()
        elif name == "NEAR":
            near_copy(j, part.at[j, other], p).start()
        elif name == "W0":
            local[0].wait()
            swapped[0].wait_recv()
        elif name == "W1":
            local[1].wait()
            swapped[1].wait_recv()
        elif name == "DZ":
            tok_copy(j, row, p, zs.at[slot, r, p], to_y).wait_send()
        elif name == "DZM":
            meta_copy(j, row, zs.at[slot, r, pieces], to_y).wait_send()
        elif name == "DY":
            tok_copy(j, y, p, ys.at[j, p], to_y).wait_send()
        elif name == "DYM":
            meta_copy(j, y, ys.at[j, pieces], to_y).wait_send()
        elif name == "DN_S":
            near_copy(j, part.at[j, other], p).wait_send()
        elif name == "DC":
            chain_copy(j, row, p, slot, to_y).wait_send()
        elif name == "OWN":
            own_copy.wait()

    def branch(m, program, low, high):
        if high - low == 1:
            for fields in program[low][0]:
                light(fields)
            return jnp.int32(packed(program[low][1]))
        half = (low + high) // 2
        return lax.cond(
            m < half, lambda: branch(m, program, low, half), lambda: branch(m, program, half, high)
        )

    def place(m, low, high):
        if high - low == 1:
            return branch(m, programs[low], 0, len(programs[low]))
        half = (low + high) // 2
        return lax.cond(z < half, lambda: place(m, low, half), lambda: place(m, half, high))

    def step(m, carry):
        word = place(m, 0, line)
        fields = []
        for size, _ in FIELDS:
            fields.append(lax.rem(word, jnp.int32(size)))
            word = lax.div(word, jnp.int32(size))
        op, j, r, p, dest, slot, f_near, f_below, f_above = fields
        row = jnp.where(r == 0, y, other)
        pl.when(op == HEAVY["UP"])(lambda: up(j, p))
        pl.when(op == HEAVY["HID"])(lambda: hidden(j))
        pl.when(op == HEAVY["DN"])(lambda: down(j, p))
        pl.when(op == HEAVY["SUM"])(lambda: sums(j, row, p, dest, slot, f_near, f_below, f_above))
        return carry

    lax.fori_loop(0, len(programs[0]), step, 0)
    for copy in swapped:
        copy.wait_send()


def on_grid(line, tokens, expert_ids, gate_weights, gate_up_weight, down_weight):
    experts = lax.axis_size("ep") * lax.axis_size("node")
    rows, width = tokens.shape
    inner = down_weight.shape[1]
    pieces = pieces_of(width)
    ag, rs = splits(line, pieces)
    order = plan(line, pieces, ag, rs)[0]
    programs = steps_of(line, pieces, ag, rs, order)
    dma, vmem, bf = pltpu.SemaphoreType.DMA, pltpu.VMEM, jnp.bfloat16
    return pl.pallas_call(
        functools.partial(kernel, line, pieces, experts, programs),
        out_shape=jax.ShapeDtypeStruct((rows, width), bf),
        in_specs=[
            pl.BlockSpec(memory_space=pltpu.VMEM),
            pl.BlockSpec(memory_space=pltpu.VMEM),
            pl.BlockSpec(memory_space=pl.ANY),
            pl.BlockSpec(memory_space=pl.ANY),
            pl.BlockSpec(memory_space=pl.ANY),
        ],
        out_specs=pl.BlockSpec(memory_space=pltpu.VMEM),
        scratch_shapes=[
            vmem((line, PAIR, rows, width), bf),
            vmem((line, PAIR, rows, LANES), bf),
            vmem((line, PAIR, rows, width), bf),
            vmem((line, rows, width), bf),
            vmem((line + 1, PAIR, rows, width), bf),
            vmem((2, width, 2 * inner), bf),
            vmem((2, inner, width), bf),
            vmem((line, 2, PAIR * rows, 2 * inner), jnp.float32),
            vmem((line, 2, PAIR * rows, inner), bf),
            vmem((line, 2, PAIR * rows, LANES), jnp.float32),
            vmem((rows, width // pieces), jnp.float32),
            dma(()), dma((2,)), dma((2,)), dma((2,)),
            dma((line, PAIR, pieces + 1)), dma((line + 1, PAIR, pieces + 1)),
            dma((line, pieces + 1)), dma((line, pieces)), dma((line, pieces)),
            dma((line + 1, PAIR, pieces)), dma((line, PAIR, pieces)),
        ],
        compiler_params=pltpu.CompilerParams(
            collective_id=0, has_side_effects=True, vmem_limit_bytes=VMEM_BYTES
        ),
    )(expert_ids, gate_weights, tokens, gate_up_weight, down_weight)


def on_device(tokens, expert_ids, gate_weights, gate_up_weight, down_weight):
    chips, cores = lax.axis_size("ep"), lax.axis_size("node")
    line = chips // PAIR
    rows, width = tokens.shape
    inner = down_weight.shape[1]
    planes = (6 * line + 3 * PAIR) * rows * width * 2 + 6 * inner * width * 2 * 1.1
    args = (tokens, expert_ids, gate_weights, gate_up_weight, down_weight)
    fits = planes < 0.9 * VMEM_BYTES and gate_up_weight.shape[0] == 1
    fits = fits and 2 * chips * cores <= LANES and pieces_of(width) > 1
    paired = cores == 2 and lax.axis_size("groups") * PAIR == 4
    if fits and paired and chips % PAIR == 0 and 1 < line < 9:
        return on_grid(line, *args)
    return spread_out(*args)


def solution(mesh):
    placed = (
        P(("groups", "ep", "node"), None),
        P(("groups", "ep", "node"), None),
        P(("groups", "ep", "node"), None),
        P(("ep", "node"), None, None),
        P(("ep", "node"), None, None),
    )
    return jax.shard_map(
        on_device,
        mesh=mesh,
        in_specs=placed,
        out_specs=P(("groups", "ep", "node"), None),
        check_vma=False,
    )
```

time: 96.2 us -> 91.5 us (0.951)
  the two profiles are of different devices: /device:TPU:0 before, /device:TPU:16 now
where the time goes in v1:
time: 91.5 us; the launch traced here: 91.1 us
  Pallas kernels  86.6 us (95%)
  local copies, waits for them, and re-layouts  4.54 us (5%)
    pallas_call x1, Pallas kernels, on_grid(): pl.pallas_call(functools.partial(kernel, line, pieces, experts, programs)...  86.6 us
    unnamed x3, local copies, waits for them, and re-layouts  4.54 us

profile of v1, /device:TPU:16, one launch (start us, length us, event | category | flops | bytes accessed | tf_op | source)
XLA Modules:
  0.0 91.1 jit_solution(6557974060720870552)
XLA Ops:
  0.0 1.4 %copy.6.ids_ref = s32[32,8]{1,0:T(8,128)} copy(s32[32,8]{0,1:T(8,128)} %param.6) | data formatting | bytes 2048 | tf_op args[1]
  1.4 1.4 %copy.7.gate_ref = f32[32,8]{1,0:T(8,128)} copy(f32[32,8]{0,1:T(8,128)} %param.7) | data formatting | bytes 2048 | tf_op args[2]
  2.7 86.6 %shard_map.55 = bf16[32,7168]{1,0:T(8,128)(2,1)} custom-call(s32[32,8]{1,0:T(8,128)} %copy.6.ids_ref, f32[32,8]{1,0:T(8,128)} %copy.7.gate_ref, bf16[32,7168]{1,0:T(8,128)(2,1)} %x_hbm.1, bf16[1,7168,512]{2,1,0:T(8,128)(2,1)} %wgu_hbm.1, bf16[1,256,7168]{2,1,0:T(8,128)(2,1)} %wd_hbm.1), custom_call_target="tpu_custom_call" | custom-call | tf_op jit(solution)/shard_map/pallas_call | solution.py:504
  89.3 1.8 %copy.9 = bf16[32,7168]{1,0:T(8,128)(2,1)} copy(bf16[32,7168]{1,0:T(8,128)(2,1)} %shard_map.55) | data formatting | bytes 917504

commit v2 on v1

--- a/solution.py
+++ b/solution.py
@@ -30,7 +30,7 @@
     return lax.psum_scatter(total.astype(jnp.bfloat16), AXES, scatter_dimension=0, tiled=True)
 
 
-RATE = dict(z=1.405, y=1.405, lat=2.1, up=0.75, dn=0.5, hid=0.4, sum=0.12, op=0.04, w0=11.0, w1=17.0, depth=2.5, meta=0.2)
+RATE = dict(z=1.46, y=1.46, lat=2.1, up=0.46, dn=0.42, hid=0.85, sum=0.2, op=0.06, w0=13.0, w1=19.0, depth=2.5, meta=0.2)
 
 def rank(style, b, top):
     if style == 'near': return b
@@ -52,6 +52,8 @@
             if op['need'] == 0: avail[op['z']].append(op)
     ops = []
     def add(z, name, deps, key, lk=None):
+        g = (z, name[0], name[1] if name[0] != 'FIN' else z, name[2] >= META if name[0] == 'AGY' else (name[4] if name[0] == 'AGZ' else 0))
+        if tweak: key = (key[0] * 100 + key[1] * 10 + tweak.get(g, 0),) + key[2:]
         op = dict(z=z, name=name, need=0, ready=0.0, key=key, link=lk)
         for d in set(deps):
             waiting.setdefault(d, []).append(op); op['need'] += 1
@@ -69,10 +71,10 @@
                 top = z if step > 0 else L-1-z
                 a = rank(style, d, top)
                 for p in list(range(P)) + [META]:
-                    for r in ((0,) if p < ag[j] or p == META else (0, 1)):
+                    for r in ((0,) if p < ag[j] else (0, 1)):
                         add(z, ('AGZ', j, r, p, lk), [('t', z, j, r, p)], (0, a, p != META, sf(p), r), lk)
             for p in list(range(P)) + [META]:
-                if p < ag[j] or p == META or j == z:
+                if p < ag[j] or j == z:
                     add(z, ('AGY', j, 0, p), [('t', z, j, 0, p)], (0, crank if j != z else -1, p != META, sf(p)), 'y')
             for p in range(P):
                 add(z, ('UP', j, p), [('t', z, j, 0, p), ('t', z, j, 1, p), ('w0', z)], (3, crank, sf(p)))
@@ -143,18 +145,54 @@
     return order, max(clock), link
 
 
+RATES7 = dict(z=1.405, y=1.405)
+MOST = 7
+AG, RS = (0.42857142857142855, 0.7142857142857143, 0.7142857142857143, 0.42857142857142855), (0.7142857142857143, 0.8571428571428571, 0.8571428571428571, 0.7142857142857143)
+SHIFTS = {
+    (0, 'AGY', 0, False): -13.36, (0, 'AGY', 0, True): -13.36, (0, 'AGY', 1, False): 55.81, (0, 'AGY', 1, True): 55.81,
+    (0, 'AGY', 2, False): -41.77, (0, 'AGY', 2, True): -41.77, (0, 'AGY', 3, False): 45.21, (0, 'AGY', 3, True): 45.21,
+    (0, 'AGZ', 0, 'd'): 249.9, (0, 'AGZ', 0, 'u'): 149.1, (0, 'AGZ', 1, 'd'): -51.32, (0, 'AGZ', 1, 'u'): 248.12,
+    (0, 'AGZ', 2, 'd'): -205.81, (0, 'AGZ', 2, 'u'): -388.16, (0, 'AGZ', 3, 'd'): 28.9, (0, 'AGZ', 3, 'u'): -24.01,
+    (0, 'DN', 0, 0): 177.24, (0, 'DN', 1, 0): 60.14, (0, 'DN', 2, 0): -31.2, (0, 'DN', 3, 0): -54.23,
+    (0, 'FIN', 0, 0): -228.62, (0, 'FIN', 1, 0): -133.78, (0, 'FIN', 2, 0): -56.6, (0, 'FIN', 3, 0): -190.02,
+    (0, 'HID', 0, 0): 158.13, (0, 'HID', 1, 0): -225.39, (0, 'HID', 2, 0): -117.65, (0, 'HID', 3, 0): -188.31,
+    (0, 'NEAR', 0, 0): 197.15, (0, 'NEAR', 1, 0): -14.44, (0, 'NEAR', 2, 0): 25.08, (0, 'NEAR', 3, 0): 57.56,
+    (0, 'SUM', 0, 0): -178.14, (0, 'SUM', 1, 0): 57.5, (0, 'SUM', 2, 0): -11.22, (0, 'SUM', 3, 0): -195.43,
+    (0, 'UP', 0, 0): -43.36, (0, 'UP', 1, 0): 93.3, (0, 'UP', 2, 0): 91.86, (0, 'UP', 3, 0): 388.72,
+    (1, 'AGY', 0, False): 7.02, (1, 'AGY', 0, True): 7.02, (1, 'AGY', 1, False): -73.06, (1, 'AGY', 1, True): -73.06,
+    (1, 'AGY', 2, False): -103.05, (1, 'AGY', 2, True): -103.05, (1, 'AGY', 3, False): -13.81, (1, 'AGY', 3, True): -13.81,
+    (1, 'AGZ', 0, 'd'): 59.55, (1, 'AGZ', 0, 'u'): 214.1, (1, 'AGZ', 1, 'd'): 139.45, (1, 'AGZ', 1, 'u'): -89.69,
+    (1, 'AGZ', 2, 'd'): 54.75, (1, 'AGZ', 2, 'u'): 14.06, (1, 'AGZ', 3, 'd'): 33.13, (1, 'AGZ', 3, 'u'): 190.08,
+    (1, 'DN', 0, 0): 207.18, (1, 'DN', 1, 0): 380.58, (1, 'DN', 2, 0): 228.14, (1, 'DN', 3, 0): -9.15,
+    (1, 'FIN', 0, 0): -45.27, (1, 'FIN', 1, 0): -130.65, (1, 'FIN', 2, 0): 97.6, (1, 'FIN', 3, 0): 118.78,
+    (1, 'HID', 0, 0): 337.71, (1, 'HID', 1, 0): -167.34, (1, 'HID', 2, 0): 364.56, (1, 'HID', 3, 0): 212.02,
+    (1, 'NEAR', 0, 0): -91.18, (1, 'NEAR', 1, 0): 89.49, (1, 'NEAR', 2, 0): -51.23, (1, 'NEAR', 3, 0): -61.51,
+    (1, 'SUM', 0, 0): 150.15, (1, 'SUM', 1, 0): 119.84, (1, 'SUM', 2, 0): -42.83, (1, 'SUM', 3, 0): -64.48,
+    (1, 'UP', 0, 0): -117.22, (1, 'UP', 1, 0): -93.07, (1, 'UP', 2, 0): -90.3, (1, 'UP', 3, 0): -53.25,
+}
+STYLE = dict(style='far', cstyle='far', rate={'z': 1.46, 'y': 1.46, 'up': 0.45999999999999996, 'dn': 0.42000000000000004, 'sum': 0.2, 'depth': 0.8}, sidefirst=False, own=1.5, tweak=None)
+
+
+def mirrored(line, shifts):
+    turned = {"u": "d", "d": "u"}
+    both = dict(shifts)
+    for (z, name, j, way), value in shifts.items():
+        both[line - 1 - z, name, line - 1 - j, turned.get(way, way)] = value
+    return both
+
+
 def pieces_of(width):
-    return max(n for n in range(1, 8) if width % (n * LANES) == 0)
+    return max(n for n in range(1, MOST + 1) if width % (n * LANES) == 0)
 
 
 def splits(line, pieces):
-    ends = round(pieces * 5 / 7)
-    return (ends,) * line, (ends,) * line
+    pick = lambda part: tuple(round(pieces * part[min(j, line - 1 - j)]) for j in range(line))
+    return pick(AG), pick(RS)
 
 
 PAIR = 2
 LANES = 128
-VMEM_BYTES = 60 * 1024 * 1024
+VMEM_BYTES = 55_900_000
 MESH = pl.DeviceIdType.MESH
 HEAVY = {"NONE": 0, "UP": 1, "HID": 2, "DN": 3, "SUM": 4}
 UP_TO, DOWN_TO, SIDE_TO, HERE = 0, 1, 2, 3
@@ -307,15 +345,14 @@
     pl.when(has_up)(lambda: greet(to_up))
     pl.when(has_dn)(lambda: greet(to_dn))
 
-    lane = lax.broadcasted_iota(jnp.int32, (rows, LANES), 1)
-    name = jnp.where(lane < experts, lane, lane - experts)
-    total = jnp.zeros((rows, LANES), jnp.float32)
-    for k in range(ids_ref.shape[1]):
-        total += jnp.where(ids_ref[:, k : k + 1] == name, gate_ref[:, k : k + 1], 0.0)
-    high = total.astype(jnp.bfloat16)
-    low = (total - high.astype(jnp.float32)).astype(jnp.bfloat16)
-    wide = jnp.where(lane < experts, high.astype(jnp.float32), low.astype(jnp.float32))
-    meta[z, y] = jnp.where(lane < 2 * experts, wide, 0.0).astype(jnp.bfloat16)
+    at_row = lax.broadcasted_iota(jnp.int32, (LANES, rows), 0)
+    name = jnp.where(at_row < experts, at_row, at_row - experts)
+    total = jnp.zeros((LANES, rows), jnp.float32)
+    for k in range(ids_ref.shape[0]):
+        total += jnp.where(ids_ref[k : k + 1, :] == name, gate_ref[k : k + 1, :], 0.0)
+    high = total.astype(jnp.bfloat16).astype(jnp.float32)
+    wide = jnp.where(at_row < experts, high, total - high)
+    meta[z, y] = jnp.where(at_row < 2 * experts, wide, 0.0).T.astype(jnp.bfloat16)
     acc[...] = jnp.zeros_like(acc)
 
     pl.semaphore_wait(barrier, 2 + jnp.where(has_up, 1, 0) + jnp.where(has_dn, 1, 0))
@@ -498,7 +535,7 @@
     inner = down_weight.shape[1]
     pieces = pieces_of(width)
     ag, rs = splits(line, pieces)
-    order = plan(line, pieces, ag, rs)[0]
+    order = plan(line, pieces, ag, rs, **dict(STYLE, tweak=mirrored(line, SHIFTS)))[0]
     programs = steps_of(line, pieces, ag, rs, order)
     dma, vmem, bf = pltpu.SemaphoreType.DMA, pltpu.VMEM, jnp.bfloat16
     return pl.pallas_call(
@@ -532,7 +569,7 @@
         compiler_params=pltpu.CompilerParams(
             collective_id=0, has_side_effects=True, vmem_limit_bytes=VMEM_BYTES
         ),
-    )(expert_ids, gate_weights, tokens, gate_up_weight, down_weight)
+    )(expert_ids.T, gate_weights.T, tokens, gate_up_weight, down_weight)
 
 
 def on_device(tokens, expert_ids, gate_weights, gate_up_weight, down_weight):

time: 91.5 us -> 77.9 us (0.85)
  the two profiles are of different devices: /device:TPU:16 before, /device:TPU:0 now
where the time goes in v2:
time: 77.9 us; the launch traced here: 77.7 us
  Pallas kernels  75.5 us (97%)
  local copies, waits for them, and re-layouts  2.14 us (3%)
    pallas_call x1, Pallas kernels, on_grid(): pl.pallas_call(functools.partial(kernel, line, pieces, experts, programs)...  75.5 us
    unnamed x5, local copies, waits for them, and re-layouts  2.14 us

profile of v2, /device:TPU:0, one launch (start us, length us, event | category | flops | bytes accessed | tf_op | source)
XLA Modules:
  0.0 77.7 jit_solution(15326427642694172514)
XLA Ops:
  0.0 0.0 copy-start
  0.0 0.7 copy-done
  0.7 0.0 copy-start.1
  0.7 0.7 copy-done.1
  1.4 75.5 %shard_map.55 = bf16[32,7168]{1,0:T(8,128)(2,1)S(1)} custom-call(s32[8,32]{1,0:T(8,128)S(1)} %bitcast.2, f32[8,32]{1,0:T(8,128)S(1)} %bitcast.3, bf16[32,7168]{1,0:T(8,128)(2,1)} %x_hbm.1, bf16[1,7168,512]{2,1,0:T(8,128)(2,1)} %wgu_hbm.1, bf16[1,256,7168]{2,1,0:T(8,128)(2,1)} %wd_hbm.1), custom_call_target="tpu_custom_call" | custom-call | tf_op jit(solution)/shard_map/pallas_call | solution.py:541
  76.9 0.8 copy.7
Async XLA Ops:
  0.0 0.7 copy-start
  0.7 0.7 copy-start.1

commit v3 on v2

--- a/solution.py
+++ b/solution.py
@@ -30,16 +30,18 @@
     return lax.psum_scatter(total.astype(jnp.bfloat16), AXES, scatter_dimension=0, tiled=True)
 
 
-RATE = dict(z=1.46, y=1.46, lat=2.1, up=0.46, dn=0.42, hid=0.85, sum=0.2, op=0.06, w0=13.0, w1=19.0, depth=2.5, meta=0.2)
+SUB = 0.3
+RATE = dict(z=1.284, y=1.284, lat=1.9, up=0.74, dn=0.63, up2=0.85, dn2=0.8, hid=0.45, sum=0.15, op=0.05, w0=11.0, w1=17.0, depth=1.5, meta=0.15)
 
 def rank(style, b, top):
     if style == 'near': return b
     if style == 'far': return top - b
     return 0 if b == 0 else top + 1 - b
 
-def plan(line, pieces, ag, rs, style='nf', cstyle='nf', rate=None, sidefirst=True, own=1.5, tweak=None):
+def plan(line, halves, pieces, ag, rs, style='nf', cstyle='nf', rate=None, sidefirst=True, own=1.5, tweak=None):
     R = dict(RATE); R.update(rate or {})
-    L, P = line, pieces
+    L, P, H = line, pieces, halves
+    B = L * H
     META = P
     time_of, waiting, avail, link, clock = {}, {}, [[] for _ in range(L)], {}, [0.0]*L
     order = [[] for _ in range(L)]
@@ -52,7 +54,7 @@
             if op['need'] == 0: avail[op['z']].append(op)
     ops = []
     def add(z, name, deps, key, lk=None):
-        g = (z, name[0], name[1] if name[0] != 'FIN' else z, name[2] >= META if name[0] == 'AGY' else (name[4] if name[0] == 'AGZ' else 0))
+        g = (z, name[0], name[1], name[4] if name[0] == 'AGZ' else '')
         if tweak: key = (key[0] * 100 + key[1] * 10 + tweak.get(g, 0),) + key[2:]
         op = dict(z=z, name=name, need=0, ready=0.0, key=key, link=lk)
         for d in set(deps):
@@ -62,43 +64,42 @@
         return op
     sf = (lambda p: -p) if sidefirst else (lambda p: p)
     for z in range(L):
-        for j in range(L):
+        for b in range(B):
+            j, h = b // H, b % H
             d = abs(j - z)
-            dist = own if d == 0 else d
-            crank = rank(cstyle, d-1, L-2) if d else own
+            crank = (rank(cstyle, d-1, L-2) if d else own) + h * SUB
             for lk, step, ends in (('u', 1, L-1), ('d', -1, 0)):
                 if z == ends or (j - z)*step > 0: continue
-                top = z if step > 0 else L-1-z
-                a = rank(style, d, top)
+                a = rank(style, d, z if step > 0 else L-1-z) + h * SUB
                 for p in list(range(P)) + [META]:
-                    for r in ((0,) if p < ag[j] else (0, 1)):
-                        add(z, ('AGZ', j, r, p, lk), [('t', z, j, r, p)], (0, a, p != META, sf(p), r), lk)
+                    for r in ((0,) if p < ag[b] else (0, 1)):
+                        add(z, ('AGZ', b, r, p, lk), [('t', z, b, r, p)], (0, a, p != META, sf(p), r), lk)
             for p in list(range(P)) + [META]:
-                if p < ag[j] or j == z:
-                    add(z, ('AGY', j, 0, p), [('t', z, j, 0, p)], (0, crank if j != z else -1, p != META, sf(p)), 'y')
+                if p < ag[b] or j == z:
+                    add(z, ('AGY', b, 0, p), [('t', z, b, 0, p)], (0, crank if j != z else -1 + h * SUB, p != META, sf(p)), 'y')
             for p in range(P):
-                add(z, ('UP', j, p), [('t', z, j, 0, p), ('t', z, j, 1, p), ('w0', z)], (3, crank, sf(p)))
-                add(z, ('DN', j, p), [('h', z, j), ('w1', z)], (2, crank, sf(p)))
-            add(z, ('HID', j), [('a', z, j, p) for p in range(P)] + [('t', z, j, 0, META), ('t', z, j, 1, META)], (2, crank, -99))
-            for p in range(rs[j]):
-                add(z, ('NEAR', j, p), [('p', z, j, p)], (1, crank, sf(p)), 'y')
+                add(z, ('UP', b, p), [('t', z, b, 0, p), ('t', z, b, 1, p), ('w0', z)], (3, crank, sf(p)))
+                add(z, ('DN', b, p), [('h', z, b), ('w1', z)], (2, crank, sf(p)))
+            add(z, ('HID', b), [('a', z, b, p) for p in range(P)] + [('t', z, b, 0, META), ('t', z, b, 1, META)], (2, crank, -99))
+            for p in range(rs[b]):
+                add(z, ('NEAR', b, p), [('p', z, b, p)], (1, crank, sf(p)), 'y')
             for p in range(P):
-                main = p < rs[j]
+                main = p < rs[b]
                 for r in ((0,) if main else (1, 0)):
-                    deps = [('p', z, j, p)]
+                    deps = [('p', z, b, p)]
                     if j == z:
-                        if z > 0: deps.append(('c', z, z, r, p))
-                        if z < L-1: deps.append(('c', z, L, r, p))
-                        if r == 0: deps.append(('n', z, z, p))
-                        add(z, ('FIN', r, p), deps, (1, -1 if r == 1 else 9, sf(p)), 'y' if r == 1 else None)
+                        if z > 0: deps.append(('c', z, b, r, p))
+                        if z < L-1: deps.append(('c', z, B + h, r, p))
+                        if r == 0: deps.append(('n', z, b, p))
+                        add(z, ('FIN', b, r, p), deps, (1, -1 if r == 1 else 9, sf(p)), 'y' if r == 1 else None)
                     else:
-                        if main: deps.append(('n', z, j, p))
-                        came = z > 0 if j > z else z < L-1
-                        if came: deps.append(('c', z, j, r, p))
-                        add(z, ('SUM', j, r, p), deps, (1, crank, sf(p), -r), 'u' if j > z else 'd')
+                        if main: deps.append(('n', z, b, p))
+                        if z > 0 if j > z else z < L-1: deps.append(('c', z, b, r, p))
+                        add(z, ('SUM', b, r, p), deps, (1, crank, sf(p), -r), 'u' if j > z else 'd')
     for z in range(L):
         for lk in 'udy': link[z, lk] = 0.0
-        for p in range(P+1): post(('t', z, z, 0, p), 0.0)
+        for h in range(H):
+            for p in range(P+1): post(('t', z, z*H + h, 0, p), 0.0)
         post(('w0', z), R['w0']); post(('w1', z), R['w1'])
     def send(z, lk, t, size):
         e = max(t, link[z, lk]) + size
@@ -125,59 +126,54 @@
             else:
                 te2 = send(z, n[4], te, size)
                 post(('t', z + (1 if n[4] == 'u' else -1), n[1], n[2], n[3]), te2)
-        elif k == 'UP':
-            te = t + R['up']; post(('a', z, n[1], n[2]), te)
+        elif k in ('UP', 'DN'):
+            done, made = ('a', 'up') if k == 'UP' else ('p', 'dn')
+            group = [op] + [o for o in cand if H == 2 and o['name'] == (k, n[1] ^ 1, n[2])]
+            te = t + R[made + ('2' if len(group) == 2 else '')]
+            for o in group:
+                post((done, z) + o['name'][1:], te)
+            if len(group) == 2:
+                avail[z].remove(group[1])
+                left -= 1
+                n = (k + '2', n[1] & ~1, n[2])
         elif k == 'HID':
             te = t + R['hid']; post(('h', z, n[1]), te)
-        elif k == 'DN':
-            te = t + R['dn']; post(('p', z, n[1], n[2]), te)
         elif k == 'NEAR':
             te = t + R['op']; post(('n', z, n[1], n[2]), send(z, 'y', te, R['y']))
         elif k == 'SUM':
-            te = t + R['sum']; up = n[1] > z; zz = z + (1 if up else -1)
-            slot = L if (zz == n[1] and not up) else n[1]
+            te = t + R['sum']; j = n[1] // H; up = j > z; zz = z + (1 if up else -1)
+            slot = B + n[1] % H if (zz == j and not up) else n[1]
             post(('c', zz, slot, n[2], n[3]), send(z, 'u' if up else 'd', te, R['z']))
         elif k == 'FIN':
             te = t + R['sum']
-            if n[1] == 1: post(('n', z, z, n[2]), send(z, 'y', te, R['y']))
+            if n[2] == 1: post(('n', z, n[1], n[3]), send(z, 'y', te, R['y']))
         clock[z] = te
         order[z].append((t, te, n))
     return order, max(clock), link
 
 
-RATES7 = dict(z=1.405, y=1.405)
-MOST = 7
-AG, RS = (0.42857142857142855, 0.7142857142857143, 0.7142857142857143, 0.42857142857142855), (0.7142857142857143, 0.8571428571428571, 0.8571428571428571, 0.7142857142857143)
+HALVES = 2
+MOST = 4
+AG, RS = (0.25, 0.75, 0.5, 0.5, 0.5, 0.5, 0.25, 0.75), (1.0, 0.5, 0.5, 1.0, 0.5, 1.0, 1.0, 0.5)
 SHIFTS = {
-    (0, 'AGY', 0, False): -13.36, (0, 'AGY', 0, True): -13.36, (0, 'AGY', 1, False): 55.81, (0, 'AGY', 1, True): 55.81,
-    (0, 'AGY', 2, False): -41.77, (0, 'AGY', 2, True): -41.77, (0, 'AGY', 3, False): 45.21, (0, 'AGY', 3, True): 45.21,
-    (0, 'AGZ', 0, 'd'): 249.9, (0, 'AGZ', 0, 'u'): 149.1, (0, 'AGZ', 1, 'd'): -51.32, (0, 'AGZ', 1, 'u'): 248.12,
-    (0, 'AGZ', 2, 'd'): -205.81, (0, 'AGZ', 2, 'u'): -388.16, (0, 'AGZ', 3, 'd'): 28.9, (0, 'AGZ', 3, 'u'): -24.01,
-    (0, 'DN', 0, 0): 177.24, (0, 'DN', 1, 0): 60.14, (0, 'DN', 2, 0): -31.2, (0, 'DN', 3, 0): -54.23,
-    (0, 'FIN', 0, 0): -228.62, (0, 'FIN', 1, 0): -133.78, (0, 'FIN', 2, 0): -56.6, (0, 'FIN', 3, 0): -190.02,
-    (0, 'HID', 0, 0): 158.13, (0, 'HID', 1, 0): -225.39, (0, 'HID', 2, 0): -117.65, (0, 'HID', 3, 0): -188.31,
-    (0, 'NEAR', 0, 0): 197.15, (0, 'NEAR', 1, 0): -14.44, (0, 'NEAR', 2, 0): 25.08, (0, 'NEAR', 3, 0): 57.56,
-    (0, 'SUM', 0, 0): -178.14, (0, 'SUM', 1, 0): 57.5, (0, 'SUM', 2, 0): -11.22, (0, 'SUM', 3, 0): -195.43,
-    (0, 'UP', 0, 0): -43.36, (0, 'UP', 1, 0): 93.3, (0, 'UP', 2, 0): 91.86, (0, 'UP', 3, 0): 388.72,
-    (1, 'AGY', 0, False): 7.02, (1, 'AGY', 0, True): 7.02, (1, 'AGY', 1, False): -73.06, (1, 'AGY', 1, True): -73.06,
-    (1, 'AGY', 2, False): -103.05, (1, 'AGY', 2, True): -103.05, (1, 'AGY', 3, False): -13.81, (1, 'AGY', 3, True): -13.81,
-    (1, 'AGZ', 0, 'd'): 59.55, (1, 'AGZ', 0, 'u'): 214.1, (1, 'AGZ', 1, 'd'): 139.45, (1, 'AGZ', 1, 'u'): -89.69,
-    (1, 'AGZ', 2, 'd'): 54.75, (1, 'AGZ', 2, 'u'): 14.06, (1, 'AGZ', 3, 'd'): 33.13, (1, 'AGZ', 3, 'u'): 190.08,
-    (1, 'DN', 0, 0): 207.18, (1, 'DN', 1, 0): 380.58, (1, 'DN', 2, 0): 228.14, (1, 'DN', 3, 0): -9.15,
-    (1, 'FIN', 0, 0): -45.27, (1, 'FIN', 1, 0): -130.65, (1, 'FIN', 2, 0): 97.6, (1, 'FIN', 3, 0): 118.78,
-    (1, 'HID', 0, 0): 337.71, (1, 'HID', 1, 0): -167.34, (1, 'HID', 2, 0): 364.56, (1, 'HID', 3, 0): 212.02,
-    (1, 'NEAR', 0, 0): -91.18, (1, 'NEAR', 1, 0): 89.49, (1, 'NEAR', 2, 0): -51.23, (1, 'NEAR', 3, 0): -61.51,
-    (1, 'SUM', 0, 0): 150.15, (1, 'SUM', 1, 0): 119.84, (1, 'SUM', 2, 0): -42.83, (1, 'SUM', 3, 0): -64.48,
-    (1, 'UP', 0, 0): -117.22, (1, 'UP', 1, 0): -93.07, (1, 'UP', 2, 0): -90.3, (1, 'UP', 3, 0): -53.25,
+    (0, 'AGY', 1, ''): -108.0, (0, 'AGY', 7, ''): -69.0, (0, 'HID', 6, ''): 30.0,
+    (0, 'NEAR', 2, ''): -139.0, (0, 'UP', 0, ''): -131.0, (0, 'UP', 2, ''): -40.0,
+    (0, 'UP', 7, ''): -45.0, (1, 'AGY', 0, ''): -116.0, (1, 'AGY', 1, ''): -148.0,
+    (1, 'AGY', 3, ''): 21.0, (1, 'AGZ', 3, 'd'): 11.0, (1, 'AGZ', 3, 'u'): -44.0,
+    (1, 'AGZ', 5, 'd'): 13.0, (1, 'DN', 3, ''): 102.0, (1, 'HID', 0, ''): 86.0,
+    (1, 'HID', 5, ''): -129.0, (1, 'NEAR', 3, ''): -85.0, (1, 'SUM', 0, ''): -69.0,
+    (1, 'SUM', 4, ''): -42.0, (1, 'UP', 0, ''): -75.0, (1, 'UP', 1, ''): 66.0,
+    (1, 'UP', 3, ''): 39.0, (1, 'UP', 7, ''): -61.0,
 }
-STYLE = dict(style='far', cstyle='far', rate={'z': 1.46, 'y': 1.46, 'up': 0.45999999999999996, 'dn': 0.42000000000000004, 'sum': 0.2, 'depth': 0.8}, sidefirst=False, own=1.5, tweak=None)
-
-
-def mirrored(line, shifts):
+STYLE = dict(style='far', cstyle='far', rate=dict(depth=1.2), sidefirst=False, own=1.5, tweak=None)
+
+
+def mirrored(line, halves, shifts):
     turned = {"u": "d", "d": "u"}
     both = dict(shifts)
-    for (z, name, j, way), value in shifts.items():
-        both[line - 1 - z, name, line - 1 - j, turned.get(way, way)] = value
+    for (z, name, b, way), value in shifts.items():
+        other = (line - 1 - b // halves) * halves + b % halves
+        both[line - 1 - z, name, other, turned.get(way, way)] = value
     return both
 
 
@@ -185,20 +181,20 @@
     return max(n for n in range(1, MOST + 1) if width % (n * LANES) == 0)
 
 
-def splits(line, pieces):
-    pick = lambda part: tuple(round(pieces * part[min(j, line - 1 - j)]) for j in range(line))
-    return pick(AG), pick(RS)
+def splits(blocks, halves, pieces):
+    last = len(AG) - 1
+    return tuple(tuple(round(pieces * part[min(b, last)]) for b in range(blocks)) for part in (AG, RS))
 
 
 PAIR = 2
 LANES = 128
 VMEM_BYTES = 55_900_000
 MESH = pl.DeviceIdType.MESH
-HEAVY = {"NONE": 0, "UP": 1, "HID": 2, "DN": 3, "SUM": 4}
+HEAVY = {"NONE": 0, "UP": 1, "HID": 2, "DN": 3, "SUM": 4, "UP2": 5, "DN2": 6}
 UP_TO, DOWN_TO, SIDE_TO, HERE = 0, 1, 2, 3
 
 
-def steps_of(line, pieces, ag, rs, order):
+def steps_of(line, halves, pieces, ag, rs, order):
     programs = []
     for z in range(line):
         steps, seen, drains = [], set(), []
@@ -213,7 +209,7 @@
             if (j, r, p) in seen:
                 return
             seen.add((j, r, p))
-            if j == z and r == 0:
+            if j // halves == z and r == 0:
                 if "own" not in seen:
                     seen.add("own")
                     emit("OWN")
@@ -235,7 +231,7 @@
                 _, j, r, p, lk = n
                 need(j, r, p)
                 dest = UP_TO if lk == "u" else DOWN_TO
-                slot = line if j == z and dest == DOWN_TO else j
+                slot = j if j // halves != z or dest == UP_TO else line * halves + j % halves
                 if p == pieces:
                     emit("AGZM", j, r, 0, dest, slot)
                     drain(start, "DZM", j, r, 0, dest, slot)
@@ -256,31 +252,37 @@
                 need(n[1], 1, n[2])
                 weight("W0")
                 emit("UP", n[1], 0, n[2])
+            elif k == "UP2":
+                for half in range(2):
+                    need(n[1] + half, 0, n[2])
+                    need(n[1] + half, 1, n[2])
+                weight("W0")
+                emit("UP2", n[1], 0, n[2])
             elif k == "HID":
                 need(n[1], 0, pieces)
                 need(n[1], 1, pieces)
                 emit("HID", n[1])
-            elif k == "DN":
+            elif k in ("DN", "DN2"):
                 weight("W1")
-                emit("DN", n[1], 0, n[2])
+                emit(k, n[1], 0, n[2])
             elif k == "NEAR":
                 emit("NEAR", n[1], 0, n[2])
                 drain(start, "DN_S", n[1], 0, n[2])
             elif k == "SUM":
                 _, j, r, p = n
-                up = j > z
-                far = j == z - 1
+                up = j // halves > z
+                far = j // halves == z - 1
                 came = z > 0 if up else z < line - 1
                 dest = UP_TO if up else DOWN_TO
-                slot = line if far else j
+                slot = line * halves + j % halves if far else j
                 emit("SUM", j, r, p, dest, slot, int(p < rs[j]), int(came))
                 drain(start, "DC", j, r, p, dest, slot)
             elif k == "FIN":
-                _, r, p = n
+                _, j, r, p = n
                 dest = SIDE_TO if r == 1 else HERE
-                emit("SUM", z, r, p, dest, z, int(r == 0), int(z > 0), int(z < line - 1))
+                emit("SUM", j, r, p, dest, j, int(r == 0), int(z > 0), int(z < line - 1))
                 if r == 1:
-                    drain(start, "DN_S", z, 0, p)
+                    drain(start, "DN_S", j, 0, p)
         for _, step in drains:
             emit(*step)
         programs.append(grouped(steps))
@@ -311,11 +313,12 @@
 
 
 def kernel(
-    line, pieces, experts, programs, ids_ref, gate_ref, x_hbm, wgu_hbm, wd_hbm, out_ref,
+    line, halves, pieces, experts, programs, ids_ref, gate_ref, x_hbm, wgu_hbm, wd_hbm, out_ref,
     tok, meta, part, near, chain, wg, wd, acc, hid, share, tot,
     x_sem, w_l, w_s, w_r, tok_r, zs, ys, near_r, near_s, chain_r, chain_s,
 ):
     rows, width = out_ref.shape
+    part_rows = rows // halves
     inner = wd.shape[1]
     block = width // pieces
     e = lax.axis_index("ep")
@@ -326,8 +329,14 @@
     to_up, to_dn = {"ep": e + PAIR}, {"ep": e - PAIR}
     to_y, to_core = {"ep": z * PAIR + other}, {"node": 1 - c}
 
-    own_copy = pltpu.make_async_copy(x_hbm, tok.at[z, y], x_sem)
-    own_copy.start()
+    own_copies = [
+        pltpu.make_async_copy(
+            x_hbm.at[pl.ds(h * part_rows, part_rows)], tok.at[z * halves + h, y], x_sem.at[h]
+        )
+        for h in range(halves)
+    ]
+    for copy in own_copies:
+        copy.start()
     local = [
         pltpu.make_async_copy(wgu_hbm.at[0], wg.at[0], w_l.at[0]),
         pltpu.make_async_copy(wd_hbm.at[0], wd.at[0], w_l.at[1]),
@@ -352,7 +361,9 @@
         total += jnp.where(ids_ref[k : k + 1, :] == name, gate_ref[k : k + 1, :], 0.0)
     high = total.astype(jnp.bfloat16).astype(jnp.float32)
     wide = jnp.where(at_row < experts, high, total - high)
-    meta[z, y] = jnp.where(at_row < 2 * experts, wide, 0.0).T.astype(jnp.bfloat16)
+    wide = jnp.where(at_row < 2 * experts, wide, 0.0).T.astype(jnp.bfloat16)
+    for h in range(halves):
+        meta[z * halves + h, y] = wide[h * part_rows : (h + 1) * part_rows]
     acc[...] = jnp.zeros_like(acc)
 
     pl.semaphore_wait(barrier, 2 + jnp.where(has_up, 1, 0) + jnp.where(has_dn, 1, 0))
@@ -400,20 +411,39 @@
 
     def up(j, p):
         at = span(p)
-        rows_in = tok[j, :, :, at].reshape(PAIR * rows, block)
+        rows_in = tok[j, :, :, at].reshape(PAIR * part_rows, block)
         for s in range(2):
             acc[j, s] += jnp.dot(rows_in, wg[s, at, :], preferred_element_type=jnp.float32)
+
+    def up_two(j, p):
+        at = span(p)
+        count = PAIR * part_rows
+        rows_in = tok[pl.ds(j, 2), :, :, at].reshape(2 * count, block)
+        for s in range(2):
+            both = jnp.dot(rows_in, wg[s, at, :], preferred_element_type=jnp.float32)
+            acc[j, s] += both[:count]
+            acc[j + 1, s] += both[count:]
+
+    def down_two(j, p):
+        at = span(p)
+        count = PAIR * part_rows
+        total = 0.0
+        for s in range(2):
+            both = jnp.concatenate([hid[j, s], hid[j + 1, s]])
+            product = jnp.dot(both, wd[s, :, at], preferred_element_type=jnp.float32)
+            total += jnp.concatenate([share[j, s, :, :1], share[j + 1, s, :, :1]]) * product
+        part[pl.ds(j, 2), :, :, at] = total.astype(jnp.bfloat16).reshape(2, PAIR, part_rows, block)
 
     def hidden(j):
         for s in range(2):
             gate, over = acc[j, s, :, :inner], acc[j, s, :, inner:]
             hid[j, s] = (jax.nn.silu(gate) * over).astype(jnp.bfloat16)
-        parts = meta[j].astype(jnp.float32).reshape(PAIR * rows, LANES)
+        parts = meta[j].astype(jnp.float32).reshape(PAIR * part_rows, LANES)
         at = lax.broadcasted_iota(jnp.int32, parts.shape, 1)
         for s, expert in enumerate(names):
             kept = jnp.where((at == expert) | (at == expert + experts), parts, 0.0)
             share[j, s] = jnp.broadcast_to(
-                jnp.sum(kept, axis=1, keepdims=True), (PAIR * rows, LANES)
+                jnp.sum(kept, axis=1, keepdims=True), (PAIR * part_rows, LANES)
             )
 
     def down(j, p):
@@ -422,10 +452,12 @@
         for s in range(2):
             product = jnp.dot(hid[j, s], wd[s, :, at], preferred_element_type=jnp.float32)
             total += share[j, s, :, :1] * product
-        part[j, :, :, at] = total.astype(jnp.bfloat16).reshape(PAIR, rows, block)
+        part[j, :, :, at] = total.astype(jnp.bfloat16).reshape(PAIR, part_rows, block)
 
     def sums(j, row, p, dest, slot, f_near, f_below, f_above):
         at = span(p)
+        half = lax.rem(j, jnp.int32(halves))
+        over = line * halves + half
         tot[...] = part[j, row, :, at].astype(jnp.float32)
 
         @pl.when(f_near == 1)
@@ -440,14 +472,14 @@
 
         @pl.when(f_above == 1)
         def _():
-            chain_copy(j, row, p, line, to_y).wait_recv()
-            tot[...] += chain[line, row, :, at].astype(jnp.float32)
+            chain_copy(j, row, p, over, to_y).wait_recv()
+            tot[...] += chain[over, row, :, at].astype(jnp.float32)
 
         value = tot[...].astype(jnp.bfloat16)
 
         @pl.when(dest == HERE)
         def _():
-            out_ref[:, at] = value
+            out_ref[pl.ds(pl.multiple_of(half * part_rows, part_rows), part_rows), at] = value
 
         @pl.when(dest != HERE)
         def _():
@@ -460,9 +492,9 @@
         row = other if r else y
         target = to_up if dest == UP_TO else to_dn
         if name == "RT":
-            tok_copy(j, row, p, x_sem, to_y).wait_recv()
+            tok_copy(j, row, p, x_sem.at[0], to_y).wait_recv()
         elif name == "RTM":
-            meta_copy(j, row, x_sem, to_y).wait_recv()
+            meta_copy(j, row, x_sem.at[0], to_y).wait_recv()
         elif name == "AGZ":
             tok_copy(j, row, p, zs.at[slot, r, p], target).start()
         elif name == "AGZM":
@@ -492,7 +524,8 @@
         elif name == "DC":
             chain_copy(j, row, p, slot, to_y).wait_send()
         elif name == "OWN":
-            own_copy.wait()
+            for copy in own_copies:
+                copy.wait()
 
     def branch(m, program, low, high):
         if high - low == 1:
@@ -521,6 +554,9 @@
         pl.when(op == HEAVY["UP"])(lambda: up(j, p))
         pl.when(op == HEAVY["HID"])(lambda: hidden(j))
         pl.when(op == HEAVY["DN"])(lambda: down(j, p))
+        if halves == 2:
+            pl.when(op == HEAVY["UP2"])(lambda: up_two(j, p))
+            pl.when(op == HEAVY["DN2"])(lambda: down_two(j, p))
         pl.when(op == HEAVY["SUM"])(lambda: sums(j, row, p, dest, slot, f_near, f_below, f_above))
         return carry
 
@@ -533,13 +569,15 @@
     experts = lax.axis_size("ep") * lax.axis_size("node")
     rows, width = tokens.shape
     inner = down_weight.shape[1]
-    pieces = pieces_of(width)
-    ag, rs = splits(line, pieces)
-    order = plan(line, pieces, ag, rs, **dict(STYLE, tweak=mirrored(line, SHIFTS)))[0]
-    programs = steps_of(line, pieces, ag, rs, order)
+    halves, pieces = HALVES, pieces_of(width)
+    blocks, part_rows = line * halves, rows // halves
+    ag, rs = splits(blocks, halves, pieces)
+    style = dict(STYLE, tweak=mirrored(line, halves, SHIFTS))
+    order = plan(line, halves, pieces, ag, rs, **style)[0]
+    programs = steps_of(line, halves, pieces, ag, rs, order)
     dma, vmem, bf = pltpu.SemaphoreType.DMA, pltpu.VMEM, jnp.bfloat16
     return pl.pallas_call(
-        functools.partial(kernel, line, pieces, experts, programs),
+        functools.partial(kernel, line, halves, pieces, experts, programs),
         out_shape=jax.ShapeDtypeStruct((rows, width), bf),
         in_specs=[
             pl.BlockSpec(memory_space=pltpu.VMEM),
@@ -550,21 +588,21 @@
         ],
         out_specs=pl.BlockSpec(memory_space=pltpu.VMEM),
         scratch_shapes=[
-            vmem((line, PAIR, rows, width), bf),
-            vmem((line, PAIR, rows, LANES), bf),
-            vmem((line, PAIR, rows, width), bf),
-            vmem((line, rows, width), bf),
-            vmem((line + 1, PAIR, rows, width), bf),
+            vmem((blocks, PAIR, part_rows, width), bf),
+            vmem((blocks, PAIR, part_rows, LANES), bf),
+            vmem((blocks, PAIR, part_rows, width), bf),
+            vmem((blocks, part_rows, width), bf),
+            vmem((blocks + halves, PAIR, part_rows, width), bf),
             vmem((2, width, 2 * inner), bf),
             vmem((2, inner, width), bf),
-            vmem((line, 2, PAIR * rows, 2 * inner), jnp.float32),
-            vmem((line, 2, PAIR * rows, inner), bf),
-            vmem((line, 2, PAIR * rows, LANES), jnp.float32),
-            vmem((rows, width // pieces), jnp.float32),
-            dma(()), dma((2,)), dma((2,)), dma((2,)),
-            dma((line, PAIR, pieces + 1)), dma((line + 1, PAIR, pieces + 1)),
-            dma((line, pieces + 1)), dma((line, pieces)), dma((line, pieces)),
-            dma((line + 1, PAIR, pieces)), dma((line, PAIR, pieces)),
+            vmem((blocks, 2, PAIR * part_rows, 2 * inner), jnp.float32),
+            vmem((blocks, 2, PAIR * part_rows, inner), bf),
+            vmem((blocks, 2, PAIR * part_rows, LANES), jnp.float32),
+            vmem((part_rows, width // pieces), jnp.float32),
+            dma((halves,)), dma((2,)), dma((2,)), dma((2,)),
+            dma((blocks, PAIR, pieces + 1)), dma((blocks + halves, PAIR, pieces + 1)),
+            dma((blocks, pieces + 1)), dma((blocks, pieces)), dma((blocks, pieces)),
+            dma((blocks + halves, PAIR, pieces)), dma((blocks, PAIR, pieces)),
         ],
         compiler_params=pltpu.CompilerParams(
             collective_id=0, has_side_effects=True, vmem_limit_bytes=VMEM_BYTES
@@ -581,6 +619,7 @@
     args = (tokens, expert_ids, gate_weights, gate_up_weight, down_weight)
     fits = planes < 0.9 * VMEM_BYTES and gate_up_weight.shape[0] == 1
     fits = fits and 2 * chips * cores <= LANES and pieces_of(width) > 1
+    fits = fits and rows % (16 * HALVES) == 0 and line * HALVES < 12
     paired = cores == 2 and lax.axis_size("groups") * PAIR == 4
     if fits and paired and chips % PAIR == 0 and 1 < line < 9:
         return on_grid(line, *args)

time: 77.9 us -> 73.9 us (0.949)
  Pallas kernels: 75.5 us -> 71.5 us
    pallas_call x1, Pallas kernels: 75.5 us -> 71.5 us  [on_grid(): pl.pallas_call(functools.partial(kernel, line, halves, pieces, experts, p...]
where the time goes in v3:
time: 73.9 us; the launch traced here: 73.7 us
  Pallas kernels  71.5 us (97%)
  local copies, waits for them, and re-layouts  2.14 us (3%)
    pallas_call x1, Pallas kernels, on_grid(): pl.pallas_call(functools.partial(kernel, line, halves, pieces, experts, p...  71.5 us
    unnamed x5, local copies, waits for them, and re-layouts  2.14 us

profile of v3, /device:TPU:0, one launch (start us, length us, event | category | flops | bytes accessed | tf_op | source)
XLA Modules:
  0.0 73.7 jit_solution(645828380265366561)
XLA Ops:
  0.0 0.0 copy-start
  0.0 0.7 copy-done
  0.7 0.0 copy-start.1
  0.7 0.7 copy-done.1
  1.4 71.5 %shard_map.55 = bf16[32,7168]{1,0:T(8,128)(2,1)S(1)} custom-call(s32[8,32]{1,0:T(8,128)S(1)} %bitcast.2, f32[8,32]{1,0:T(8,128)S(1)} %bitcast.3, bf16[32,7168]{1,0:T(8,128)(2,1)} %x_hbm.1, bf16[1,7168,512]{2,1,0:T(8,128)(2,1)} %wgu_hbm.1, bf16[1,256,7168]{2,1,0:T(8,128)(2,1)} %wd_hbm.1), custom_call_target="tpu_custom_call" | custom-call | tf_op jit(solution)/shard_map/pallas_call | solution.py:579
  72.9 0.8 %copy.7 = bf16[32,7168]{1,0:T(8,128)(2,1)} copy(bf16[32,7168]{1,0:T(8,128)(2,1)S(1)} %shard_map.55) | data formatting | bytes 917504
Async XLA Ops:
  0.0 0.7 copy-start
  0.7 0.7 copy-start.1

commit v4 on v3

--- a/solution.py
+++ b/solution.py
@@ -31,7 +31,7 @@
 
 
 SUB = 0.3
-RATE = dict(z=1.284, y=1.284, lat=1.9, up=0.74, dn=0.63, up2=0.85, dn2=0.8, hid=0.45, sum=0.15, op=0.05, w0=11.0, w1=17.0, depth=1.5, meta=0.15)
+RATE = dict(z=1.284, y=1.284, lat=1.9, up=0.74, dn=0.63, up2=0.85, dn2=0.8, hid=0.45, sum=0.15, op=0.05, w0=11.0, w1=17.0, depth=1.5, meta=0.23)
 
 def rank(style, b, top):
     if style == 'near': return b
@@ -71,16 +71,16 @@
             for lk, step, ends in (('u', 1, L-1), ('d', -1, 0)):
                 if z == ends or (j - z)*step > 0: continue
                 a = rank(style, d, z if step > 0 else L-1-z) + h * SUB
-                for p in list(range(P)) + [META]:
+                for p in list(range(P)) + [META] * (h == 0):
                     for r in ((0,) if p < ag[b] else (0, 1)):
                         add(z, ('AGZ', b, r, p, lk), [('t', z, b, r, p)], (0, a, p != META, sf(p), r), lk)
-            for p in list(range(P)) + [META]:
+            for p in list(range(P)) + [META] * (h == 0):
                 if p < ag[b] or j == z:
                     add(z, ('AGY', b, 0, p), [('t', z, b, 0, p)], (0, crank if j != z else -1 + h * SUB, p != META, sf(p)), 'y')
             for p in range(P):
                 add(z, ('UP', b, p), [('t', z, b, 0, p), ('t', z, b, 1, p), ('w0', z)], (3, crank, sf(p)))
                 add(z, ('DN', b, p), [('h', z, b), ('w1', z)], (2, crank, sf(p)))
-            add(z, ('HID', b), [('a', z, b, p) for p in range(P)] + [('t', z, b, 0, META), ('t', z, b, 1, META)], (2, crank, -99))
+            add(z, ('HID', b), [('a', z, b, p) for p in range(P)] + [('t', z, j*H, 0, META), ('t', z, j*H, 1, META)], (2, crank, -99))
             for p in range(rs[b]):
                 add(z, ('NEAR', b, p), [('p', z, b, p)], (1, crank, sf(p)), 'y')
             for p in range(P):
@@ -156,14 +156,54 @@
 MOST = 4
 AG, RS = (0.25, 0.75, 0.5, 0.5, 0.5, 0.5, 0.25, 0.75), (1.0, 0.5, 0.5, 1.0, 0.5, 1.0, 1.0, 0.5)
 SHIFTS = {
-    (0, 'AGY', 1, ''): -108.0, (0, 'AGY', 7, ''): -69.0, (0, 'HID', 6, ''): 30.0,
-    (0, 'NEAR', 2, ''): -139.0, (0, 'UP', 0, ''): -131.0, (0, 'UP', 2, ''): -40.0,
-    (0, 'UP', 7, ''): -45.0, (1, 'AGY', 0, ''): -116.0, (1, 'AGY', 1, ''): -148.0,
-    (1, 'AGY', 3, ''): 21.0, (1, 'AGZ', 3, 'd'): 11.0, (1, 'AGZ', 3, 'u'): -44.0,
-    (1, 'AGZ', 5, 'd'): 13.0, (1, 'DN', 3, ''): 102.0, (1, 'HID', 0, ''): 86.0,
-    (1, 'HID', 5, ''): -129.0, (1, 'NEAR', 3, ''): -85.0, (1, 'SUM', 0, ''): -69.0,
-    (1, 'SUM', 4, ''): -42.0, (1, 'UP', 0, ''): -75.0, (1, 'UP', 1, ''): 66.0,
-    (1, 'UP', 3, ''): 39.0, (1, 'UP', 7, ''): -61.0,
+    (0, 'AGY', 0, ''): 75.74, (0, 'AGY', 1, ''): -107.52, (0, 'AGY', 2, ''): 93.39,
+    (0, 'AGY', 3, ''): 122.46, (0, 'AGY', 4, ''): -1.56, (0, 'AGY', 5, ''): -184.63,
+    (0, 'AGY', 6, ''): -3.66, (0, 'AGY', 7, ''): -68.82, (0, 'AGZ', 0, 'd'): 10.21,
+    (0, 'AGZ', 0, 'u'): 58.64, (0, 'AGZ', 1, 'd'): 90.19, (0, 'AGZ', 1, 'u'): 74.78,
+    (0, 'AGZ', 2, 'd'): 83.79, (0, 'AGZ', 2, 'u'): 125.7, (0, 'AGZ', 3, 'd'): -5.37,
+    (0, 'AGZ', 3, 'u'): -62.66, (0, 'AGZ', 4, 'd'): -158.02, (0, 'AGZ', 4, 'u'): -144.91,
+    (0, 'AGZ', 5, 'd'): 66.06, (0, 'AGZ', 5, 'u'): 37.48, (0, 'AGZ', 6, 'd'): -126.18,
+    (0, 'AGZ', 6, 'u'): -192.65, (0, 'AGZ', 7, 'd'): -31.03, (0, 'AGZ', 7, 'u'): -2.99,
+    (0, 'DN', 0, ''): 30.47, (0, 'DN', 1, ''): 178.94, (0, 'DN', 2, ''): 10.51,
+    (0, 'DN', 3, ''): 67.83, (0, 'DN', 4, ''): -35.99, (0, 'DN', 5, ''): 27.04,
+    (0, 'DN', 6, ''): 23.23, (0, 'DN', 7, ''): -20.52, (0, 'FIN', 0, ''): -53.87,
+    (0, 'FIN', 1, ''): 49.76, (0, 'FIN', 2, ''): -9.79, (0, 'FIN', 3, ''): 25.25,
+    (0, 'FIN', 4, ''): -111.85, (0, 'FIN', 5, ''): -34.61, (0, 'FIN', 6, ''): 23.62,
+    (0, 'FIN', 7, ''): 40.9, (0, 'HID', 0, ''): -10.3, (0, 'HID', 1, ''): -71.55,
+    (0, 'HID', 2, ''): -46.61, (0, 'HID', 3, ''): 62.94, (0, 'HID', 4, ''): 23.54,
+    (0, 'HID', 5, ''): 12.69, (0, 'HID', 6, ''): 30.34, (0, 'HID', 7, ''): -18.5,
+    (0, 'NEAR', 0, ''): 33.99, (0, 'NEAR', 1, ''): 33.86, (0, 'NEAR', 2, ''): -138.54,
+    (0, 'NEAR', 3, ''): -29.78, (0, 'NEAR', 4, ''): 49.06, (0, 'NEAR', 5, ''): 58.77,
+    (0, 'NEAR', 6, ''): 86.66, (0, 'NEAR', 7, ''): 21.99, (0, 'SUM', 0, ''): -27.77,
+    (0, 'SUM', 1, ''): 16.47, (0, 'SUM', 2, ''): 58.91, (0, 'SUM', 3, ''): -67.76,
+    (0, 'SUM', 4, ''): -32.45, (0, 'SUM', 5, ''): 7.77, (0, 'SUM', 6, ''): -120.03,
+    (0, 'SUM', 7, ''): 13.54, (0, 'UP', 0, ''): -130.65, (0, 'UP', 1, ''): 142.4,
+    (0, 'UP', 2, ''): -40.31, (0, 'UP', 3, ''): -12.29, (0, 'UP', 4, ''): -68.57,
+    (0, 'UP', 5, ''): 10.47, (0, 'UP', 6, ''): 7.16, (0, 'UP', 7, ''): -44.69,
+    (1, 'AGY', 0, ''): -115.63, (1, 'AGY', 1, ''): -147.53, (1, 'AGY', 2, ''): -5.18,
+    (1, 'AGY', 3, ''): 20.69, (1, 'AGY', 4, ''): 23.6, (1, 'AGY', 5, ''): 61.08,
+    (1, 'AGY', 6, ''): -108.08, (1, 'AGY', 7, ''): -0.23, (1, 'AGZ', 0, 'd'): 84.61,
+    (1, 'AGZ', 0, 'u'): -47.23, (1, 'AGZ', 1, 'd'): -110.73, (1, 'AGZ', 1, 'u'): -9.49,
+    (1, 'AGZ', 2, 'd'): -5.64, (1, 'AGZ', 2, 'u'): 25.14, (1, 'AGZ', 3, 'd'): 10.69,
+    (1, 'AGZ', 3, 'u'): -44.08, (1, 'AGZ', 4, 'd'): -34.64, (1, 'AGZ', 4, 'u'): 25.54,
+    (1, 'AGZ', 5, 'd'): 12.74, (1, 'AGZ', 5, 'u'): 26.21, (1, 'AGZ', 6, 'd'): -30.75,
+    (1, 'AGZ', 6, 'u'): 110.32, (1, 'AGZ', 7, 'd'): -37.55, (1, 'AGZ', 7, 'u'): -100.64,
+    (1, 'DN', 0, ''): 5.73, (1, 'DN', 1, ''): -117.79, (1, 'DN', 2, ''): -122.16,
+    (1, 'DN', 3, ''): 102.39, (1, 'DN', 4, ''): -19.51, (1, 'DN', 5, ''): 41.63,
+    (1, 'DN', 6, ''): -61.83, (1, 'DN', 7, ''): 6.53, (1, 'FIN', 0, ''): 16.64,
+    (1, 'FIN', 1, ''): 30.82, (1, 'FIN', 2, ''): -87.38, (1, 'FIN', 3, ''): 5.63,
+    (1, 'FIN', 4, ''): 142.35, (1, 'FIN', 5, ''): 11.19, (1, 'FIN', 6, ''): -70.69,
+    (1, 'FIN', 7, ''): -35.7, (1, 'HID', 0, ''): 86.41, (1, 'HID', 1, ''): -126.17,
+    (1, 'HID', 2, ''): -25.6, (1, 'HID', 3, ''): -18.73, (1, 'HID', 4, ''): -13.15,
+    (1, 'HID', 5, ''): -128.66, (1, 'HID', 6, ''): -46.31, (1, 'HID', 7, ''): 4.65,
+    (1, 'NEAR', 0, ''): -67.58, (1, 'NEAR', 1, ''): 17.99, (1, 'NEAR', 2, ''): -39.22,
+    (1, 'NEAR', 3, ''): -84.68, (1, 'NEAR', 4, ''): -43.47, (1, 'NEAR', 5, ''): 150.74,
+    (1, 'NEAR', 6, ''): -24.69, (1, 'NEAR', 7, ''): -101.06, (1, 'SUM', 0, ''): -68.57,
+    (1, 'SUM', 1, ''): 297.99, (1, 'SUM', 2, ''): 62.81, (1, 'SUM', 3, ''): 29.89,
+    (1, 'SUM', 4, ''): -41.77, (1, 'SUM', 5, ''): 89.48, (1, 'SUM', 6, ''): -110.69,
+    (1, 'SUM', 7, ''): -16.09, (1, 'UP', 0, ''): -75.26, (1, 'UP', 1, ''): 66.45,
+    (1, 'UP', 2, ''): -48.19, (1, 'UP', 3, ''): 38.78, (1, 'UP', 4, ''): 16.03,
+    (1, 'UP', 5, ''): 30.82, (1, 'UP', 6, ''): 3.65, (1, 'UP', 7, ''): -61.06,
 }
 STYLE = dict(style='far', cstyle='far', rate=dict(depth=1.2), sidefirst=False, own=1.5, tweak=None)
 
@@ -259,8 +299,8 @@
                 weight("W0")
                 emit("UP2", n[1], 0, n[2])
             elif k == "HID":
-                need(n[1], 0, pieces)
-                need(n[1], 1, pieces)
+                need(n[1] // halves * halves, 0, pieces)
+                need(n[1] // halves * halves, 1, pieces)
                 emit("HID", n[1])
             elif k in ("DN", "DN2"):
                 weight("W1")
@@ -391,7 +431,7 @@
         return remote(ref, ref, s, tok_r.at[j, row, p], target)
 
     def meta_copy(j, row, s, target):
-        ref = meta.at[j, row]
+        ref = meta.at[pl.ds(j, halves), row]
         return remote(ref, ref, s, tok_r.at[j, row, pieces], target)
 
     def both_ways(dest, act):

time: 73.9 us -> 74.8 us (1.012)
  Pallas kernels: 71.5 us -> 72.4 us
    pallas_call x1, Pallas kernels: 71.5 us -> 72.4 us  [on_grid(): pl.pallas_call(functools.partial(kernel, line, halves, pieces, experts, p...]
where the time goes in v4:
time: 74.8 us; the launch traced here: 74.6 us
  Pallas kernels  72.4 us (97%)
  local copies, waits for them, and re-layouts  2.14 us (3%)
    pallas_call x1, Pallas kernels, on_grid(): pl.pallas_call(functools.partial(kernel, line, halves, pieces, experts, p...  72.4 us
    unnamed x5, local copies, waits for them, and re-layouts  2.14 us

profile of v4, /device:TPU:0, one launch (start us, length us, event | category | flops | bytes accessed | tf_op | source)
XLA Modules:
  0.0 74.6 jit_solution(16448653193526243916)
XLA Ops:
  0.0 0.0 copy-start
  0.0 0.7 copy-done
  0.7 0.0 copy-start.1
  0.7 0.7 copy-done.1
  1.4 72.4 %shard_map.55 = bf16[32,7168]{1,0:T(8,128)(2,1)S(1)} custom-call(s32[8,32]{1,0:T(8,128)S(1)} %bitcast.2, f32[8,32]{1,0:T(8,128)S(1)} %bitcast.3, bf16[32,7168]{1,0:T(8,128)(2,1)} %x_hbm.1, bf16[1,7168,512]{2,1,0:T(8,128)(2,1)} %wgu_hbm.1, bf16[1,256,7168]{2,1,0:T(8,128)(2,1)} %wd_hbm.1), custom_call_target="tpu_custom_call" | custom-call | tf_op jit(solution)/shard_map/pallas_call | solution.py:619
  73.8 0.8 %copy.7 = bf16[32,7168]{1,0:T(8,128)(2,1)} copy(bf16[32,7168]{1,0:T(8,128)(2,1)S(1)} %shard_map.55) | data formatting | bytes 917504
Async XLA Ops:
  0.0 0.7 copy-start
  0.7 0.7 copy-start.1
